TPU v7x, 512 devices: a whole 4x8x8 slice. The times are simulated.
512 devices in a mesh: dp: 128 (over z, y, core), group: 4 (over x).
Axes of the slice: x: 4, y: 8, z: 8, core: 2. Of those that a mesh axis runs over, the one named last changes fastest.
Arguments:
- features: bfloat16 [65536, 512], P(('dp', 'group')), may hold values from -6 to 6
- head_weight: bfloat16 [512, 512], replicated, may hold values from -0.25 to 0.25
- owner_of_image: int32 [65536, 1], P(('dp', 'group')), may hold values from 0 to 127; in each aligned block of 128 rows (0 to 127, 128 to 255, ...) at most 2 rows name the same one
- class_slot: int32 [65536], P(('dp', 'group')), may hold values from 0 to 49
- is_query: int32 [65536], P(('dp', 'group')), may hold values 0 or 1
- episode_ways: int32 [512], P(('dp', 'group')), may hold values from 5 to 50
Outputs:
- grad_features: bfloat16 [65536, 512], P(('dp', 'group'))
- grad_weight: float32 [512, 512], replicated
- losses: float32 [512], P(('dp', 'group'))
Inputs may be any that keep to these rules, and one draw needn't show every extreme that they name: `owner_of_image`: among the rows of one device at most 2 name any one owner, a bound that some block reaches.
All inputs are finite; a program needn't handle non-finite values. No bound on the sum of `is_query` on one device may be relied on, other than what follows from the above.
Results may differ from a plain program's by a relative error of at most 0.0037.
The roundings to bfloat16 on the way count: a program that leaves them out, or rounds other values in their place, can miss the bound.
Values may be sent and summed in bfloat16 or wider, within the bound.
A program may use at most 64 MiB of HBM per device.

v0:
```python
import jax
import jax.numpy as jnp
from jax import lax
from jax.sharding import Mesh
from jax.sharding import PartitionSpec as P

D = 512
WAYS_MAX = 50
DP = ("dp_0", "dp_1", "dp_2")
DP_GROUP = ("dp_0", "dp_1", "dp_2", "group")


def filled_up(lines, count):
    spare = -lines.shape[0] % count
    if not spare:
        return lines
    return jnp.concatenate([lines, jnp.zeros((spare, *lines.shape[1:]), lines.dtype)])


def from_everyone(value, axis):
    count = lax.axis_size(axis)
    return lax.all_to_all(
        jnp.broadcast_to(value[None], (count, *value.shape)), axis, 0, 0, tiled=True
    )


def laid_out(parts, dim):
    lengths = list(parts.shape[1:])
    lengths[dim] *= parts.shape[0]
    return jnp.moveaxis(parts, 0, dim).reshape(lengths)


def gather_axes(value, axes, dim):
    far, near = axes
    initial = from_everyone(value, far)
    parts = jnp.swapaxes(from_everyone(initial, near), 0, 1)
    return laid_out(parts.reshape(-1, *value.shape), dim)


def split_up(value, dim, count):
    before, after = (value.shape[:dim], value.shape[dim + 1 :])
    return jnp.moveaxis(value.reshape(*before, count, -1, *after), dim, 0)


def sent_and_summed(value, axis, dim):
    parts = split_up(value, dim, lax.axis_size(axis))
    arrived = lax.all_to_all(parts, axis, split_axis=0, concat_axis=0, tiled=True)
    return arrived.sum(axis=0)


def sum_in_two_steps(value, axes, dim):
    far, near = axes
    own = sent_and_summed(split_up(value, dim, lax.axis_size(far)), near, dim + 1)
    return jnp.sum(lax.all_to_all(own, far, 0, 0, tiled=True), axis=0)


def nested_sum(value, axes):
    lines = value.reshape(-1, value.shape[-1])
    padded = filled_up(lines, lax.axis_size(axes[0]) * lax.axis_size(axes[1]))
    whole = gather_axes(sum_in_two_steps(padded, axes, 0), axes, 0)
    return lax.slice_in_dim(whole, 0, len(lines)).reshape(value.shape)


def episode_losses(embeds, codes, ways_table):
    count_ep = ways_table.shape[0]
    is_live = codes > 0
    code_value = jnp.maximum(codes - 1, 0)
    query_rows = is_live & (code_value % 2 == 1)
    support_rows = is_live & (code_value % 2 == 0)
    slot_value = code_value // 2
    episode = slot_value // WAYS_MAX
    raw_class = slot_value % WAYS_MAX
    episode_hot = episode[:, None] == jnp.arange(count_ep, dtype=jnp.int32)[None, :]
    row_ways = jnp.sum(jnp.where(episode_hot, ways_table[None, :], 0), axis=1)
    label_id = episode * WAYS_MAX + raw_class % row_ways
    classes = jnp.arange(count_ep * WAYS_MAX, dtype=jnp.int32)
    class_hot = label_id[:, None] == classes[None, :]
    support_hot = (class_hot & support_rows[:, None]).astype(jnp.float32)
    counts = jnp.sum(support_hot, axis=0)
    class_sums = jnp.dot(support_hot.T, embeds, precision=lax.Precision.HIGHEST)
    prototypes = class_sums / jnp.maximum(counts, 1.0)[:, None]
    class_ways = jnp.repeat(ways_table, WAYS_MAX)
    class_valid = classes % WAYS_MAX < class_ways
    allowed = (episode[:, None] == (classes // WAYS_MAX)[None, :]) & class_valid[None, :]
    cross_term = jnp.dot(embeds, prototypes.T, precision=lax.Precision.HIGHEST)
    distance = (
        jnp.sum(embeds * embeds, axis=1)[:, None]
        - 2.0 * cross_term
        + jnp.sum(prototypes * prototypes, axis=1)[None, :]
    )
    scores = -distance * D ** (-0.5)
    masked = jnp.where(allowed, scores, -1e30)
    row_max = jnp.max(masked, axis=1, keepdims=True)
    log_total = row_max[:, 0] + jnp.log(jnp.sum(jnp.exp(masked - row_max), axis=1))
    picked = jnp.sum(jnp.where(class_hot, scores, 0.0), axis=1)
    per_query = jnp.where(query_rows, log_total - picked, 0.0)
    hot_float = episode_hot.astype(jnp.float32)
    query_count = jnp.sum(hot_float * query_rows[:, None].astype(jnp.float32), axis=0)
    return jnp.sum(hot_float * per_query[:, None], axis=0) / jnp.maximum(query_count, 1.0)


def times_transpose(left, right):
    return lax.dot_general(
        left, right, (((1,), (1,)), ((), ())), preferred_element_type=jnp.float32
    )


def inner_rows(left, right):
    return lax.dot_general(
        left, right, (((0,), (0,)), ((), ())), preferred_element_type=jnp.float32
    )


def on_device(features, head_weight, owner_of_image, class_slot, is_query, episode_ways):
    peers = lax.axis_size(DP)
    row_count = features.shape[0]
    capacity = 2 * row_count // peers
    target = owner_of_image[:, 0]
    one_hot = (target[:, None] == jnp.arange(peers, dtype=jnp.int32)[None, :]).astype(jnp.int32)
    before = jnp.cumsum(one_hot, axis=0) - one_hot
    position = jnp.sum(one_hot * before, axis=1)
    flat_slot = target * capacity + position
    codes = class_slot * 2 + is_query + 1
    send_rows = (
        jnp.zeros((peers * capacity, D), jnp.bfloat16)
        .at[flat_slot]
        .set(features)
        .reshape(peers, capacity, D)
    )
    send_codes = (
        jnp.zeros((peers * capacity,), jnp.int32).at[flat_slot].set(codes).reshape(peers, capacity)
    )
    got_rows, got_codes = (
        lax.all_to_all(send_rows, DP, split_axis=0, concat_axis=0, tiled=True),
        lax.all_to_all(send_codes, DP, split_axis=0, concat_axis=0, tiled=True),
    )
    got_rows = got_rows.reshape(peers * capacity, D)
    got_codes = got_codes.reshape(peers * capacity)
    got_embeds = jnp.dot(got_rows, head_weight, preferred_element_type=jnp.float32).astype(
        jnp.bfloat16
    )
    losses, pull = jax.vjp(
        lambda e: episode_losses(e, got_codes, episode_ways), got_embeds.astype(jnp.float32)
    )
    grad_embeds = pull(jnp.ones_like(losses))[0].astype(jnp.bfloat16)
    partial_value = inner_rows(got_rows, grad_embeds)
    outgoing = times_transpose(grad_embeds, head_weight).astype(jnp.bfloat16)
    returned = lax.all_to_all(
        outgoing.reshape(peers, capacity, D), DP, split_axis=0, concat_axis=0, tiled=True
    )
    own_rows = returned.reshape(peers * capacity, D)[flat_slot]
    grad_weight = nested_sum(partial_value, (("dp_0", "dp_1"), ("dp_2", "group")))
    return (own_rows, grad_weight, losses)


def solution(mesh):
    split = Mesh(
        mesh.devices.reshape(8, 8, 2, mesh.shape["group"]), ("dp_0", "dp_1", "dp_2", "group")
    )
    placed = (P(DP_GROUP, None), P(), P(DP_GROUP, None), P(DP_GROUP), P(DP_GROUP), P(DP_GROUP))
    return jax.shard_map(
        on_device,
        mesh=split,
        in_specs=placed,
        out_specs=(P(DP_GROUP, None), P(), P(DP_GROUP)),
        check_vma=False,
    )
```

profile of v0, /device:TPU:1, one launch (start us, length us, event | category | flops | bytes accessed | tf_op | source)
XLA Modules:
  0.0 159.2 jit_solution(10938305493173677287)
XLA Ops:
  0.7 0.7 copy-done.1
  1.4 0.2 reduce_window_sum.11
  1.6 0.2 select_reduce_fusion
  1.8 0.6 copy-done.2
  2.5 1.0 scatter_custom_fusion.1
  3.5 0.8 all_to_all.25
  4.2 18.4 %all-to-all-start.1 = ((s32[128,1,2]{2,1,0:T(1,128)}), s32[128,1,2]{2,1,0:T(1,128)S(1)}, u32[]{:S(2)}, u32[]{:S(2)}) async-start(s32[128,1,2]{2,1,0:T(1,128)} %bitcast.3), calls=%async_computation.1 | async-start | bytes 131072 | tf_op jit(solution)/shard_map/all_to_all | solution.py:135
  23.3 1.5 scatter_custom_fusion
  24.8 0.8 reshape.207
  25.6 8.4 %all-to-all-done.1 = s32[128,1,2]{2,1,0:T(1,128)S(1)} async-done(((s32[128,1,2]{2,1,0:T(1,128)}), s32[128,1,2]{2,1,0:T(1,128)S(1)}, u32[]{:S(2)}, u32[]{:S(2)}) %all-to-all-start.1) | async-done | bytes 1056 | tf_op jit(solution)/shard_map/all_to_all | solution.py:135
  34.1 5.7 %all-to-all-start = ((bf16[128,2,512]{2,1,0:T(2,128)(2,1)}), bf16[128,2,512]{2,1,0:T(2,128)(2,1)S(1)}, u32[]{:S(2)}, u32[]{:S(2)}) async-start(bf16[128,2,512]{2,1,0:T(2,128)(2,1)} %reshape.207), calls=%async_computation | async-start | bytes 524288 | tf_op jit(solution)/shard_map/all_to_all | solution.py:134
  39.9 0.1 copy.30
  40.1 0.1 gt.20
  40.2 0.1 copy.26
  40.4 0.2 ne.195
  40.6 0.1 rem.80
  40.9 0.1 div.75
  41.0 0.1 fusion.27
  41.2 0.1 convert_reduce_fusion.1
  41.3 13.8 %all-to-all-done = bf16[128,2,512]{2,1,0:T(2,128)(2,1)S(1)} async-done(((bf16[128,2,512]{2,1,0:T(2,128)(2,1)}), bf16[128,2,512]{2,1,0:T(2,128)(2,1)S(1)}, u32[]{:S(2)}, u32[]{:S(2)}) %all-to-all-start) | async-done | bytes 262176 | tf_op jit(solution)/shard_map/all_to_all | solution.py:134
  55.3 0.1 copy.31
  55.4 0.4 fusion.6
  55.8 0.3 multiply_reduce_fusion
  56.1 0.4 fusion.34
  56.6 0.1 sub.62
  56.8 0.6 select_reduce_fusion.2
  58.1 0.1 multiply_reduce_fusion.3
  58.3 0.2 multiply_reduce_fusion.1
  58.5 0.3 fusion.1
  58.8 0.6 convolution_add_fusion.1
  59.4 0.4 fusion
  59.8 0.3 convolution_bitcast_fusion
  60.1 0.6 copy.32
  60.7 19.4 %all_to_all.39 = f32[8,64,1,512]{3,1,2,0:T(8,128)S(1)} all-to-all(f32[8,64,1,512]{3,1,2,0:T(8,128)S(1)} %copy.32), channel_id=1, replica_groups=mesh['dp_0'=8,'dp_1'=8,'dp_2'=2,'group'=4] {'dp_2','group'}, dimensions={0} | all-to-all | bytes 2097152 | tf_op jit(solution)/shard_map/all_to_all | solution.py:47
  80.4 15.5 %all_to_all.40 = f32[64,1,512]{2,1,0:T(1,128)S(1)} all-to-all(f32[64,1,512]{2,1,0:T(1,128)S(1)} %reduce_sum.162), channel_id=1, replica_groups=mesh['dp_0'=8,'dp_1'=8,'dp_2'=2,'group'=4] {'dp_0','dp_1'}, dimensions={0} | all-to-all | bytes 262144 | tf_op jit(solution)/shard_map/all_to_all | solution.py:54
  95.9 0.1 reduce_sum.163
  96.0 0.7 broadcast_in_dim.94
  96.7 4.8 %all-to-all-start.5 = ((f32[64,1,512]{2,1,0:T(1,128)}), f32[64,1,512]{2,1,0:T(1,128)S(1)}, u32[]{:S(2)}, u32[]{:S(2)}) async-start(f32[64,1,512]{2,1,0:T(1,128)} %broadcast_in_dim.94), calls=%async_computation.5 | async-start | bytes 262144 | tf_op jit(solution)/shard_map/all_to_all | solution.py:22
  101.5 0.3 convolution_convert_fusion
  101.9 0.8 reshape.210
  102.7 10.2 %all-to-all-done.5 = f32[64,1,512]{2,1,0:T(1,128)S(1)} async-done(((f32[64,1,512]{2,1,0:T(1,128)}), f32[64,1,512]{2,1,0:T(1,128)S(1)}, u32[]{:S(2)}, u32[]{:S(2)}) %all-to-all-start.5) | async-done | bytes 131104 | tf_op jit(solution)/shard_map/all_to_all | solution.py:22
  112.9 8.3 %all-to-all-start.2 = ((bf16[128,2,512]{2,1,0:T(2,128)(2,1)}), bf16[128,2,512]{2,1,0:T(2,128)(2,1)S(1)}, u32[]{:S(2)}, u32[]{:S(2)}) async-start(bf16[128,2,512]{2,1,0:T(2,128)(2,1)} %reshape.210), calls=%async_computation.2 | async-start | bytes 524288 | tf_op jit(solution)/shard_map/all_to_all | solution.py:148
  121.2 15.3 %all-to-all-done.2 = bf16[128,2,512]{2,1,0:T(2,128)(2,1)S(1)} async-done(((bf16[128,2,512]{2,1,0:T(2,128)(2,1)}), bf16[128,2,512]{2,1,0:T(2,128)(2,1)S(1)}, u32[]{:S(2)}, u32[]{:S(2)}) %all-to-all-start.2) | async-done | bytes 262176 | tf_op jit(solution)/shard_map/all_to_all | solution.py:148
  136.5 1.1 broadcast_in_dim.96
  137.6 3.9 %all-to-all-start.6 = ((f32[8,64,1,512]{3,1,2,0:T(8,128)}), f32[8,64,1,512]{3,1,2,0:T(8,128)S(1)}, u32[]{:S(2)}, u32[]{:S(2)}) async-start(f32[8,64,1,512]{3,1,2,0:T(8,128)} %broadcast_in_dim.96), calls=%async_computation.6 | async-start | bytes 2097152 | tf_op jit(solution)/shard_map/all_to_all | solution.py:22
  142.3 1.5 gather_fusion
  143.8 12.7 %all-to-all-done.6 = f32[8,64,1,512]{3,1,2,0:T(8,128)S(1)} async-done(((f32[8,64,1,512]{3,1,2,0:T(8,128)}), f32[8,64,1,512]{3,1,2,0:T(8,128)S(1)}, u32[]{:S(2)}, u32[]{:S(2)}) %all-to-all-start.6) | async-done | bytes 1048608 | tf_op jit(solution)/shard_map/all_to_all | solution.py:22
  156.5 1.6 copy.38
  (32 shorter events, 1.1 us)
Async XLA Ops:
  0.6 54.8 %copy-start = (bf16[512,512]{1,0:T(8,128)(2,1)S(1)}, bf16[512,512]{1,0:T(8,128)(2,1)}, u32[]{:S(2)}) copy-start(bf16[512,512]{1,0:T(8,128)(2,1)} %param.7) | copy-start | bytes 1572868
  0.6 0.7 copy-start.1
  1.8 0.7 copy-start.2
  1.8 0.7 copy-start.3
  4.2 29.8 %all-to-all-start.1 = ((s32[128,1,2]{2,1,0:T(1,128)}), s32[128,1,2]{2,1,0:T(1,128)S(1)}, u32[]{:S(2)}, u32[]{:S(2)}) async-start(s32[128,1,2]{2,1,0:T(1,128)} %bitcast.3), calls=%async_computation.1 | async-start | bytes 131072 | tf_op jit(solution)/shard_map/all_to_all | solution.py:135
  34.1 21.1 %all-to-all-start = ((bf16[128,2,512]{2,1,0:T(2,128)(2,1)}), bf16[128,2,512]{2,1,0:T(2,128)(2,1)S(1)}, u32[]{:S(2)}, u32[]{:S(2)}) async-start(bf16[128,2,512]{2,1,0:T(2,128)(2,1)} %reshape.207), calls=%async_computation | async-start | bytes 524288 | tf_op jit(solution)/shard_map/all_to_all | solution.py:134
  96.7 16.2 %all-to-all-start.5 = ((f32[64,1,512]{2,1,0:T(1,128)}), f32[64,1,512]{2,1,0:T(1,128)S(1)}, u32[]{:S(2)}, u32[]{:S(2)}) async-start(f32[64,1,512]{2,1,0:T(1,128)} %broadcast_in_dim.94), calls=%async_computation.5 | async-start | bytes 262144 | tf_op jit(solution)/shard_map/all_to_all | solution.py:22
  112.9 23.7 %all-to-all-start.2 = ((bf16[128,2,512]{2,1,0:T(2,128)(2,1)}), bf16[128,2,512]{2,1,0:T(2,128)(2,1)S(1)}, u32[]{:S(2)}, u32[]{:S(2)}) async-start(bf16[128,2,512]{2,1,0:T(2,128)(2,1)} %reshape.210), calls=%async_computation.2 | async-start | bytes 524288 | tf_op jit(solution)/shard_map/all_to_all | solution.py:148
  137.6 18.8 %all-to-all-start.6 = ((f32[8,64,1,512]{3,1,2,0:T(8,128)}), f32[8,64,1,512]{3,1,2,0:T(8,128)S(1)}, u32[]{:S(2)}, u32[]{:S(2)}) async-start(f32[8,64,1,512]{3,1,2,0:T(8,128)} %broadcast_in_dim.96), calls=%async_computation.6 | async-start | bytes 2097152 | tf_op jit(solution)/shard_map/all_to_all | solution.py:22
where the time goes:
time: 160 us; the launch traced here: 159 us
  waiting for transfers between devices  60.5 us (38%)
  starting transfers between devices  41.1 us (26%)
  blocking collectives  34.9 us (22%)
  local copies, waits for them, and re-layouts  13.5 us (8%)
  between operations  4.05 us (3%)
  matrix products  2.98 us (2%)
  other arithmetic  2.08 us (1%)
    all_to_all x2, waiting for transfers between devices, from_everyone(): lax.all_to_all(jnp.broadcast_to(value[None], (count, *value.shape)), axis...  22.9 us
    all_to_all x1, blocking collectives, sent_and_summed(): lax.all_to_all(parts, axis, split_axis=0, concat_axis=0, tiled=True)  19.4 us
    all_to_all x1, starting transfers between devices, on_device(): lax.all_to_all(send_codes, DP, split_axis=0, concat_axis=0, tiled=True)  18.4 us
    all_to_all x1, blocking collectives, sum_in_two_steps(): return jnp.sum(lax.all_to_all(own, far, 0, 0, tiled=True), axis=0)  15.5 us
    all_to_all x1, waiting for transfers between devices, on_device(): lax.all_to_all(outgoing.reshape(peers, capacity, D), DP, split_axis=0, co...  15.3 us
    all_to_all x1, waiting for transfers between devices, on_device(): lax.all_to_all(send_rows, DP, split_axis=0, concat_axis=0, tiled=True)  13.8 us
    all_to_all x2, starting transfers between devices, from_everyone(): lax.all_to_all(jnp.broadcast_to(value[None], (count, *value.shape)), axis...  8.66 us
    all_to_all x1, waiting for transfers between devices, on_device(): lax.all_to_all(send_codes, DP, split_axis=0, concat_axis=0, tiled=True)  8.43 us
  transfers between devices with their start and end apart: 5, of which 5 were waited for; matrix products, arithmetic and copies ran while one was open for 4% of the time, Pallas kernels for 0%

commit v1 on v0

v1 whole, which is shorter than its diff:
```python
import functools

import jax
import jax.numpy as jnp
from jax import lax
from jax.experimental import pallas as pl
from jax.experimental.pallas import tpu as pltpu
from jax.sharding import PartitionSpec as P

D = 512
WAYS_MAX = 50
CLASSES = 64
CAP = 2
LANES = 128
MESH = pl.DeviceIdType.MESH
F32 = jnp.float32
BF16 = jnp.bfloat16
I32 = jnp.int32


def dot(a, b, ca, cb):
    return lax.dot_general(a, b, (((ca,), (cb,)), ((), ())), preferred_element_type=F32)


def iota(shape, dim):
    return lax.broadcasted_iota(I32, shape, dim)


def three_parts(x):
    hi = x.astype(BF16)
    rest = x - hi.astype(F32)
    mid = rest.astype(BF16)
    low = (rest - mid.astype(F32)).astype(BF16)
    return hi, mid, low


def to_lanes(column):
    n = column.shape[0]
    same = iota((n, n), 0) == iota((n, n), 1)
    return jnp.sum(jnp.where(same, column, 0.0), axis=0, keepdims=True)


def to_sublanes(row):
    n = row.shape[1]
    same = iota((n, n), 0) == iota((n, n), 1)
    return jnp.sum(jnp.where(same, row, 0.0), axis=1, keepdims=True)


def episode(rows, codes, ways, weight):
    count = rows.shape[0]
    embeds = dot(rows, weight, 1, 0).astype(BF16)
    wide = embeds.astype(F32)
    code = codes.astype(I32)
    value = jnp.maximum(code - 1, 0)
    live = code > 0
    odd = lax.rem(value, 2) == 1
    query = (live & odd).astype(F32)
    label = lax.div(value, 2)
    for factor in (8, 4, 2, 1):
        label = jnp.where(label >= factor * ways, label - factor * ways, label)
    classes = iota((CLASSES, count), 0)
    hot = classes == label
    support = jnp.where(hot & live & jnp.logical_not(odd), 1.0, 0.0)
    counts = jnp.maximum(jnp.sum(support, axis=1, keepdims=True), 1.0)
    support = support.astype(BF16)
    protos = dot(support, embeds, 1, 0) / counts
    parts = three_parts(protos)
    crosses = dot(jnp.concatenate(parts, axis=0), embeds, 1, 1)
    cross = crosses[:CLASSES] + crosses[CLASSES : 2 * CLASSES] + crosses[2 * CLASSES :]
    norm_e = to_lanes(jnp.sum(wide * wide, axis=1, keepdims=True))
    norm_p = jnp.sum(protos * protos, axis=1, keepdims=True)
    distance = norm_e - 2.0 * cross + norm_p
    scores = -distance * D ** (-0.5)
    masked = jnp.where(classes < ways, scores, -1e30)
    top = jnp.max(masked, axis=0, keepdims=True)
    powers = jnp.exp(masked - top)
    total = jnp.sum(powers, axis=0, keepdims=True)
    picked = jnp.sum(jnp.where(hot, scores, 0.0), axis=0, keepdims=True)
    per_query = jnp.where(query > 0.0, top + jnp.log(total) - picked, 0.0)
    queries = jnp.maximum(jnp.sum(query, axis=1, keepdims=True), 1.0)
    loss = jnp.sum(per_query, axis=1, keepdims=True) / queries
    share = query / queries
    by_dist = (jnp.where(hot, 1.0, 0.0) - powers / total) * (share * D ** (-0.5))
    by_parts = three_parts(by_dist)
    pulls = dot(jnp.concatenate(by_parts, axis=0), embeds, 1, 0)
    pull = pulls[:CLASSES] + pulls[CLASSES : 2 * CLASSES] + pulls[2 * CLASSES :]
    by_sums = 2.0 * (protos * jnp.sum(by_dist, axis=1, keepdims=True) - pull) / counts
    sum_parts = three_parts(by_sums)
    left = jnp.concatenate([by_parts[0], by_parts[0], by_parts[1], support, support], axis=0)
    right = jnp.concatenate(
        [-2.0 * parts[0], -2.0 * parts[1], -2.0 * parts[0], sum_parts[0], sum_parts[1]], axis=0
    )
    own = to_sublanes(jnp.sum(by_dist, axis=0, keepdims=True))
    grads = dot(left, right, 0, 0) + 2.0 * own * wide
    return grads.astype(BF16), loss


def kernel(
    n,
    n_group,
    owner_ref,
    slot_ref,
    query_ref,
    ways_ref,
    features_ref,
    weight_hbm,
    out_rows_ref,
    out_weight_ref,
    out_loss_ref,
    weight_ref,
    rows_send,
    rows_recv,
    back_send,
    back_recv,
    halves,
    fold_send,
    fold_recv,
    part_send,
    part_recv,
    cross_send,
    cross_recv,
    whole,
    load_sem,
    rows_ss,
    rows_rs,
    back_ss,
    back_rs,
    fold_ss,
    fold_rs,
    part_ss,
    part_rs,
    cross_ss,
    cross_rs,
    whole_ss,
    whole_rs,
    twin_ss,
    twin_rs,
):
    me = lax.axis_index("dp")
    group = lax.axis_index("group")
    chips = n // 2
    core = lax.rem(me, 2)
    chip = lax.div(me, 2)
    twin = me + 1 - 2 * core
    rows = features_ref.shape[0]
    half = D // 2

    barrier = pltpu.get_barrier_semaphore()

    def greet(step, carry):
        peer = lax.rem(me + step, n)
        pl.semaphore_signal(barrier, inc=1, device_id=(peer, group), device_id_type=MESH)
        return carry

    def greet_group(step, carry):
        peer = lax.rem(group + step, n_group)
        pl.semaphore_signal(barrier, inc=1, device_id=(me, peer), device_id_type=MESH)
        return carry

    lax.fori_loop(1, n, greet, 0)
    lax.fori_loop(1, n_group, greet_group, 0)
    load = pltpu.make_async_copy(weight_hbm, weight_ref, load_sem)
    load.start()

    owner = owner_ref[...].astype(F32)
    owner_lane = to_lanes(owner)
    earlier = (owner == owner_lane) & (iota((rows, rows), 0) < iota((rows, rows), 1))
    place = jnp.sum(jnp.where(earlier, 1.0, 0.0), axis=0, keepdims=True)
    slot = (owner_lane * CAP + place).astype(I32)
    hot = iota((n * CAP, rows), 0) == slot
    codes = (slot_ref[...] * 2 + query_ref[...] + 1).astype(F32)
    code_column = jnp.sum(jnp.where(hot, codes, 0.0), axis=1, keepdims=True)
    hot = jnp.where(hot, 1.0, 0.0).astype(BF16)
    packed = dot(hot, features_ref[...], 1, 0).astype(BF16)
    code_tile = jnp.broadcast_to(code_column, (n * CAP, LANES)).astype(BF16)
    rows_send[...] = jnp.concatenate([packed, code_tile], axis=1).reshape(rows_send.shape)
    rows_recv[me] = rows_send[me]

    pl.semaphore_wait(barrier, n + n_group - 2)

    def send_rows(step, carry):
        peer = lax.rem(me + step, n)
        pltpu.make_async_remote_copy(
            src_ref=rows_send.at[peer],
            dst_ref=rows_recv.at[me],
            send_sem=rows_ss,
            recv_sem=rows_rs,
            device_id=(peer, group),
            device_id_type=MESH,
        ).start()
        return carry

    lax.fori_loop(1, n, send_rows, 0)
    load.wait()
    others = rows_recv.at[pl.ds(0, n - 1)]
    pltpu.make_async_copy(others, others, rows_rs).wait()

    got = rows_recv[...].reshape(n * CAP, D + LANES)
    got_rows = got[:, :D]
    first = jnp.where(iota((8, LANES), 1) == 0, 1.0, 0.0).astype(BF16)
    got_codes = dot(first, got[:, D:], 1, 1)[:1]
    grads, loss = episode(got_rows, got_codes, ways_ref[0], weight_ref[...])
    out_loss_ref[...] = loss

    for part in range(2):
        halves[part] = got_rows[:, part * half : (part + 1) * half]

    def term(which):
        value = dot(halves[which], grads, 0, 0)
        return jnp.concatenate(
            [value[:, i * LANES : (i + 1) * LANES] for i in range(D // LANES)], axis=0
        )

    fold_send[...] = term(1 - core).astype(BF16)
    fold = pltpu.make_async_remote_copy(
        src_ref=fold_send,
        dst_ref=fold_recv,
        send_sem=fold_ss,
        recv_sem=fold_rs,
        device_id=(twin, group),
        device_id_type=MESH,
    )
    fold.start()
    own = term(core)
    outgoing = dot(grads, weight_ref[...], 1, 1).astype(BF16)
    back_send[...] = outgoing.reshape(back_send.shape)
    back_recv[me] = back_send[me]
    fold.wait_recv()
    part_send[...] = (own + fold_recv[...].astype(F32)).astype(BF16).reshape(part_send.shape)
    part_recv[chip] = part_send[chip]

    def send_part(step, carry):
        peer = lax.rem(chip + step, chips)
        pltpu.make_async_remote_copy(
            src_ref=part_send.at[peer],
            dst_ref=part_recv.at[chip],
            send_sem=part_ss,
            recv_sem=part_rs,
            device_id=(2 * peer + core, group),
            device_id_type=MESH,
        ).start()
        return carry

    def send_back(step, carry):
        peer = lax.rem(me + step, n)
        pltpu.make_async_remote_copy(
            src_ref=back_send.at[peer],
            dst_ref=back_recv.at[me],
            send_sem=back_ss,
            recv_sem=back_rs,
            device_id=(peer, group),
            device_id_type=MESH,
        ).start()
        return carry

    lax.fori_loop(1, chips, send_part, 0)
    lax.fori_loop(1, n, send_back, 0)
    others = part_recv.at[pl.ds(0, chips - 1)]
    pltpu.make_async_copy(others, others, part_rs).wait()
    cross_send[...] = jnp.sum(part_recv[...].astype(F32), axis=0)
    cross_recv[group] = cross_send[...]

    def send_cross(step, carry):
        peer = lax.rem(group + step, n_group)
        pltpu.make_async_remote_copy(
            src_ref=cross_send,
            dst_ref=cross_recv.at[group],
            send_sem=cross_ss,
            recv_sem=cross_rs,
            device_id=(me, peer),
            device_id_type=MESH,
        ).start()
        return carry

    lax.fori_loop(1, n_group, send_cross, 0)
    others = cross_recv.at[pl.ds(0, n_group - 1)]
    pltpu.make_async_copy(others, others, cross_rs).wait()
    whole[core, chip] = jnp.sum(cross_recv[...], axis=0).astype(BF16)

    def send_whole(step, carry):
        peer = lax.rem(chip + step, chips)
        pltpu.make_async_remote_copy(
            src_ref=whole.at[core, chip],
            dst_ref=whole.at[core, chip],
            send_sem=whole_ss,
            recv_sem=whole_rs,
            device_id=(2 * peer + core, group),
            device_id_type=MESH,
        ).start()
        return carry

    lax.fori_loop(1, chips, send_whole, 0)

    others = back_recv.at[pl.ds(0, n - 1)]
    pltpu.make_async_copy(others, others, back_rs).wait()
    returned = back_recv[...].reshape(n * CAP, D)
    out_rows_ref[...] = dot(hot, returned, 0, 0).astype(BF16)

    others = whole.at[0, pl.ds(0, chips - 1)]
    pltpu.make_async_copy(others, others, whole_rs).wait()
    last = pltpu.make_async_remote_copy(
        src_ref=whole.at[core],
        dst_ref=whole.at[core],
        send_sem=twin_ss,
        recv_sem=twin_rs,
        device_id=(twin, group),
        device_id_type=MESH,
    )
    last.start()
    sent = rows_send.at[pl.ds(0, n - 1)]
    pltpu.make_async_copy(sent, sent, rows_ss).wait()
    sent = back_send.at[pl.ds(0, n - 1)]
    pltpu.make_async_copy(sent, sent, back_ss).wait()
    sent = part_send.at[pl.ds(0, chips - 1)]
    pltpu.make_async_copy(sent, sent, part_ss).wait()
    sent = whole.at[0, pl.ds(0, chips - 1)]
    pltpu.make_async_copy(sent, sent, whole_ss).wait()
    sent = cross_recv.at[pl.ds(0, n_group - 1)]
    pltpu.make_async_copy(sent, sent, cross_ss).wait()
    fold.wait_send()
    last.wait()
    out_weight_ref[...] = whole[...]


def on_device(n, n_group, features, weight, owner, slots, queries, ways):
    rows = features.shape[0]
    chips = n // 2
    lines = D * D // 2 // LANES
    vmem = pl.BlockSpec(memory_space=pltpu.VMEM)
    dma = pltpu.SemaphoreType.DMA
    part = (chips, lines // chips, LANES)
    own_rows, terms, losses = pl.pallas_call(
        functools.partial(kernel, n, n_group),
        out_shape=(
            jax.ShapeDtypeStruct((rows, D), BF16),
            jax.ShapeDtypeStruct((2, *part), BF16),
            jax.ShapeDtypeStruct((1, 1), F32),
        ),
        in_specs=[
            vmem,
            vmem,
            vmem,
            pl.BlockSpec(memory_space=pltpu.SMEM),
            vmem,
            pl.BlockSpec(memory_space=pl.ANY),
        ],
        out_specs=(vmem, vmem, vmem),
        scratch_shapes=[
            pltpu.VMEM((D, D), BF16),
            pltpu.VMEM((n, CAP, D + LANES), BF16),
            pltpu.VMEM((n, CAP, D + LANES), BF16),
            pltpu.VMEM((n, CAP, D), BF16),
            pltpu.VMEM((n, CAP, D), BF16),
            pltpu.VMEM((2, n * CAP, D // 2), BF16),
            pltpu.VMEM((lines, LANES), BF16),
            pltpu.VMEM((lines, LANES), BF16),
            pltpu.VMEM(part, BF16),
            pltpu.VMEM(part, BF16),
            pltpu.VMEM(part[1:], F32),
            pltpu.VMEM((n_group, *part[1:]), F32),
            pltpu.VMEM((2, *part), BF16),
        ]
        + [dma] * 15,
        compiler_params=pltpu.CompilerParams(collective_id=0, has_side_effects=True),
        name="episodes",
    )(owner, slots.reshape(1, rows), queries.reshape(1, rows), ways, features, weight)
    blocks = terms.reshape(2, D // LANES, D // 2, LANES)
    grad_weight = jnp.swapaxes(blocks, 1, 2).reshape(D, D).astype(F32)
    return own_rows, grad_weight, losses.reshape(1)


def solution(mesh):
    both = P(("dp", "group"))
    lines = P(("dp", "group"), None)
    return jax.shard_map(
        functools.partial(on_device, mesh.shape["dp"], mesh.shape["group"]),
        mesh=mesh,
        in_specs=(lines, P(), lines, both, both, both),
        out_specs=(lines, P(), both),
        check_vma=False,
    )
```

time: 160 us -> 70.1 us (0.44)
  Pallas kernels: 0 us -> 61.9 us
  waiting for transfers between devices: 60.5 us -> 0 us
  starting transfers between devices: 41.1 us -> 0 us
  blocking collectives: 34.9 us -> 0 us
  local copies, waits for them, and re-layouts: 13.5 us -> 3.76 us
  matrix products: 2.98 us -> 0 us
    pallas_call x0 -> x1, Pallas kernels: none -> 61.9 us  [on_device(): pl.pallas_call(functools.partial(kernel, n, n_group), out_shape=(jax.Shap...]
    all_to_all x5 -> x0, waiting for transfers between devices: 60.5 us -> none  [the longest x2 22.9 us: from_everyone(): lax.all_to_all(jnp.broadcast_to(value[None], (count, *value.shape)), axis...]
    all_to_all x5 -> x0, starting transfers between devices: 41.1 us -> none  [the longest x1 18.4 us: on_device(): lax.all_to_all(send_codes, DP, split_axis=0, concat_axis=0, tiled=True)]
    all_to_all x2 -> x0, blocking collectives: 34.9 us -> none  [the longest x1 19.4 us: sent_and_summed(): lax.all_to_all(parts, axis, split_axis=0, concat_axis=0, tiled=True)]
    dot_general x8 -> x0, matrix products: 2.98 us -> none  [the longest x3 1.27 us: episode_losses(): cross_term = jnp.dot(embeds, prototypes.T, precision=lax.Precision.HIGHEST)]
    scatter x2 -> x0, local copies, waits for them, and re-layouts: 2.48 us -> none  [the longest x1 1.5 us: on_device(): send_rows = jnp.zeros((peers * capacity, D), jnp.bfloat16).at[flat_slot]....]
    all_to_all x3 -> x0, local copies, waits for them, and re-layouts: 2.41 us -> none  [the longest x1 1.58 us: from_everyone(): lax.all_to_all(jnp.broadcast_to(value[None], (count, *value.shape)), axis...]
    broadcast_in_dim x2 -> x0, local copies, waits for them, and re-layouts: 1.82 us -> none  [from_everyone(): jnp.broadcast_to(value[None], (count, *value.shape))]
  transfers between devices with their start and end apart: 5 -> 0, of which waited for: 5 -> 0; matrix products, arithmetic and copies ran while one was open for 4% -> 0% of each run, Pallas kernels for 0% -> 0%
where the time goes in v1:
time: 70.1 us; the launch traced here: 69.8 us
  Pallas kernels  61.9 us (88%)
  local copies, waits for them, and re-layouts  3.76 us (5%)
  between operations  3.02 us (4%)
  other arithmetic  1.11 us (2%)
    pallas_call x1, Pallas kernels, on_device(): pl.pallas_call(functools.partial(kernel, n, n_group), out_shape=(jax.Shap...  61.9 us
    unnamed x7, local copies, waits for them, and re-layouts  3.09 us

profile of v1, /device:TPU:1, one launch (start us, length us, event | category | flops | bytes accessed | tf_op | source)
XLA Modules:
  0.0 69.8 jit_solution(11061534866084844256)
XLA Ops:
  1.3 0.0 copy-start.1
  1.3 0.6 copy-done.1
  1.9 0.7 %copy.9.owner_ref = s32[128,1]{1,0:T(8,128)} copy(s32[128,1]{0,1:T(1,128)S(1)} %copy-done.1) | data formatting | bytes 1024 | tf_op args[2]
  2.7 61.9 %episodes.1 = (bf16[128,512]{1,0:T(8,128)(2,1)}, bf16[2,64,16,128]{3,2,1,0:T(8,128)(2,1)}, f32[1,1]{1,0:T(1,128)}) custom-call(s32[128,1]{1,0:T(8,128)} %copy.9.owner_ref, s32[1,128]{1,0:T(1,128)} %bitcast.17, s32[1,128]{1,0:T(1,128)} %bitcast.18, s32[1]{0:T(128)S(6)} %copy.16.ways_ref, bf16[128,512]{1,0:T(8,128)(2,1)} %features_ref.1, ...), custom_call_target="tpu_custom_call" | custom-call | tf_op jit(solution)/shard_map/episodes/pallas_call | solution.py:332
  64.6 1.1 %convert_bitcast_fusion = f32[2,256,4,128]{3,1,2,0:T(8,128)S(1)} fusion(bf16[2,4,256,128]{3,2,1,0:T(8,128)(2,1)} %bitcast.16), kind=kLoop, calls=%fused_computation.1 | loop fusion | flops 262144 | bytes 1572864 | tf_op jit(solution)/shard_map/convert_element_type | solution.py:368
  65.7 0.7 copy.10
  66.4 0.0 copy-start
  66.4 1.0 %copy.13 = f32[64,8,4,128]{3,1,2,0:T(8,128)} copy(f32[64,8,4,128]{3,2,1,0:T(4,128)S(1)} %bitcast.14) | data formatting | bytes 2097152
  67.5 0.0 copy-done
  67.5 0.7 copy.17
Async XLA Ops:
  1.3 0.7 copy-start.1
  66.4 1.1 %copy-start = (bf16[128,512]{1,0:T(8,128)(2,1)S(1)}, bf16[128,512]{1,0:T(8,128)(2,1)}, u32[]{:S(2)}) copy-start(bf16[128,512]{1,0:T(8,128)(2,1)} %get-tuple-element.12) | copy-start | bytes 393220

commit v2 on v1

v2 whole, which is shorter than its diff:
```python
import functools
import math

import jax
import jax.numpy as jnp
from jax import lax
from jax.experimental import pallas as pl
from jax.experimental.pallas import tpu as pltpu
from jax.sharding import PartitionSpec as P

D = 512
WAYS_MAX = 50
CLASSES = 64
CAP = 2
LANES = 128
MESH = pl.DeviceIdType.MESH
F32 = jnp.float32
BF16 = jnp.bfloat16
I32 = jnp.int32
BACK = (0, 0)


def dot(a, b, ca, cb):
    return lax.dot_general(a, b, (((ca,), (cb,)), ((), ())), preferred_element_type=F32)


def iota(shape, dim):
    return lax.broadcasted_iota(I32, shape, dim)


def three_parts(x):
    hi = x.astype(BF16)
    rest = x - hi.astype(F32)
    mid = rest.astype(BF16)
    low = (rest - mid.astype(F32)).astype(BF16)
    return hi, mid, low


def to_lanes(column):
    n = column.shape[0]
    same = iota((n, n), 0) == iota((n, n), 1)
    return jnp.sum(jnp.where(same, column, 0.0), axis=0, keepdims=True)


def to_sublanes(row):
    n = row.shape[1]
    same = iota((n, n), 0) == iota((n, n), 1)
    return jnp.sum(jnp.where(same, row, 0.0), axis=1, keepdims=True)


def episode(rows, codes, ways, weight):
    count = rows.shape[0]
    embeds = dot(rows, weight, 1, 0).astype(BF16)
    wide = embeds.astype(F32)
    code = codes.astype(I32)
    value = jnp.maximum(code - 1, 0)
    live = code > 0
    odd = lax.rem(value, 2) == 1
    query = (live & odd).astype(F32)
    label = lax.div(value, 2)
    for factor in (8, 4, 2, 1):
        label = jnp.where(label >= factor * ways, label - factor * ways, label)
    classes = iota((CLASSES, count), 0)
    hot = classes == label
    support = jnp.where(hot & live & jnp.logical_not(odd), 1.0, 0.0)
    counts = jnp.maximum(jnp.sum(support, axis=1, keepdims=True), 1.0)
    support = support.astype(BF16)
    protos = dot(support, embeds, 1, 0) / counts
    parts = three_parts(protos)
    crosses = dot(jnp.concatenate(parts, axis=0), embeds, 1, 1)
    cross = crosses[:CLASSES] + crosses[CLASSES : 2 * CLASSES] + crosses[2 * CLASSES :]
    norm_e = to_lanes(jnp.sum(wide * wide, axis=1, keepdims=True))
    norm_p = jnp.sum(protos * protos, axis=1, keepdims=True)
    distance = norm_e - 2.0 * cross + norm_p
    scores = -distance * D ** (-0.5)
    masked = jnp.where(classes < ways, scores, -1e30)
    top = jnp.max(masked, axis=0, keepdims=True)
    powers = jnp.exp(masked - top)
    total = jnp.sum(powers, axis=0, keepdims=True)
    picked = jnp.sum(jnp.where(hot, scores, 0.0), axis=0, keepdims=True)
    per_query = jnp.where(query > 0.0, top + jnp.log(total) - picked, 0.0)
    queries = jnp.maximum(jnp.sum(query, axis=1, keepdims=True), 1.0)
    loss = jnp.sum(per_query, axis=1, keepdims=True) / queries
    share = query / queries
    by_dist = (jnp.where(hot, 1.0, 0.0) - powers / total) * (share * D ** (-0.5))
    by_parts = three_parts(by_dist)
    pulls = dot(jnp.concatenate(by_parts, axis=0), embeds, 1, 0)
    pull = pulls[:CLASSES] + pulls[CLASSES : 2 * CLASSES] + pulls[2 * CLASSES :]
    by_sums = 2.0 * (protos * jnp.sum(by_dist, axis=1, keepdims=True) - pull) / counts
    sum_parts = three_parts(by_sums)
    left = jnp.concatenate([by_parts[0], by_parts[0], by_parts[1], support, support], axis=0)
    right = jnp.concatenate(
        [-2.0 * parts[0], -2.0 * parts[1], -2.0 * parts[0], sum_parts[0], sum_parts[1]], axis=0
    )
    own = to_sublanes(jnp.sum(by_dist, axis=0, keepdims=True))
    grads = dot(left, right, 0, 0) + 2.0 * own * wide
    return grads.astype(BF16), loss


def farthest_first(count):
    return sorted(range(count), key=lambda i: -min(i, count - i))


def arrived(block, sem):
    pltpu.make_async_copy(block, block, sem).wait()


def lay_out(blocks, out_ref, which):
    lines = out_ref.shape[0] // 2
    value = blocks[which].reshape(D // LANES, lines, LANES)
    start = pl.multiple_of(which * lines, lines)
    for i in range(D // LANES):
        out_ref[pl.ds(start, lines), i * LANES : (i + 1) * LANES] = value[i].astype(F32)


def kernel(
    n,
    n_group,
    owner_hbm,
    slot_hbm,
    query_hbm,
    ways_hbm,
    features_hbm,
    weight_hbm,
    out_rows_ref,
    out_weight_ref,
    out_loss_ref,
    owner_ref,
    slot_ref,
    query_ref,
    ways_ref,
    features_ref,
    weight_ref,
    rows_send,
    rows_recv,
    back_send,
    back_recv,
    halves,
    fold_send,
    fold_recv,
    part_send,
    part_recv,
    line_send,
    line_recv,
    cross_send,
    cross_recv,
    whole,
    load_sem,
    rows_ss,
    rows_rs,
    back_ss,
    back_rs,
    fold_ss,
    fold_rs,
    part_ss,
    part_rs,
    line_ss,
    line_rs,
    cross_ss,
    cross_rs,
    whole_ss,
    whole_rs,
    twin_ss,
    twin_rs,
):
    me = lax.axis_index("dp")
    group = lax.axis_index("group")
    chips = n // 2
    side = math.isqrt(chips)
    core = lax.rem(me, 2)
    chip = lax.div(me, 2)
    high = lax.div(chip, side)
    low = lax.rem(chip, side)
    twin = me + 1 - 2 * core
    rows = features_ref.shape[0]
    half = D // 2
    offsets = farthest_first(side)
    highs = [lax.rem(high + i, side) * (2 * side) for i in range(side)]
    lows = [lax.rem(low + i, side) * 2 for i in range(side)]
    groups = [lax.rem(group + i, n_group) for i in range(1, n_group)]
    plane = [(h, w) for h in offsets for w in offsets if h or w]
    row_peers = [highs[h] + lows[w] + c for h, w in plane for c in range(2)] + [twin]
    lines = [
        (low, [(lax.rem(low + i, side), highs[0] + lows[i] + core) for i in offsets if i]),
        (high, [(lax.rem(high + i, side), highs[i] + lows[0] + core) for i in offsets if i]),
    ]

    barrier = pltpu.get_barrier_semaphore()
    with jax.named_scope("greet"):
        for peer in row_peers:
            pl.semaphore_signal(barrier, inc=1, device_id=(peer, group), device_id_type=MESH)
        for peer in groups:
            pl.semaphore_signal(barrier, inc=1, device_id=(me, peer), device_id_type=MESH)
    loads = [
        pltpu.make_async_copy(source, target, load_sem.at[i])
        for i, (source, target) in enumerate(
            (
                (owner_hbm, owner_ref),
                (features_hbm, features_ref),
                (slot_hbm, slot_ref),
                (query_hbm, query_ref),
                (ways_hbm, ways_ref),
                (weight_hbm, weight_ref),
            )
        )
    ]
    for load in loads:
        load.start()
    for load in loads:
        load.wait()

    owner_lane = owner_ref[...].astype(F32)
    owner = to_sublanes(owner_lane)
    earlier = (owner == owner_lane) & (iota((rows, rows), 0) < iota((rows, rows), 1))
    place = jnp.sum(jnp.where(earlier, 1.0, 0.0), axis=0, keepdims=True)
    slot = (owner_lane * CAP + place).astype(I32)
    hot = iota((n * CAP, rows), 0) == slot
    codes = (slot_ref[...] * 2 + query_ref[...] + 1).astype(F32)
    code_column = jnp.sum(jnp.where(hot, codes, 0.0), axis=1, keepdims=True)
    hot = jnp.where(hot, 1.0, 0.0).astype(BF16)
    packed = dot(hot, features_ref[...], 1, 0).astype(BF16)
    code_tile = jnp.broadcast_to(code_column, (n * CAP, LANES)).astype(BF16)
    rows_send[...] = jnp.concatenate([packed, code_tile], axis=1).reshape(rows_send.shape)
    rows_recv[me] = rows_send[me]

    with jax.named_scope("barrier_wait"):
        pl.semaphore_wait(barrier, n + n_group - 2)

    with jax.named_scope("send_rows"):
        for peer in row_peers:
            pltpu.make_async_remote_copy(
                src_ref=rows_send.at[peer],
                dst_ref=rows_recv.at[me],
                send_sem=rows_ss,
                recv_sem=rows_rs,
                device_id=(peer, group),
                device_id_type=MESH,
            ).start()
    others = rows_recv.at[pl.ds(0, n - 1)]
    with jax.named_scope("rows_wait"):
        pltpu.make_async_copy(others, others, rows_rs).wait()

    got = rows_recv[...].reshape(n * CAP, D + LANES)
    got_rows = got[:, :D]
    first = jnp.where(iota((8, LANES), 1) == 0, 1.0, 0.0).astype(BF16)
    got_codes = dot(first, got[:, D:], 1, 1)[:1]
    with jax.named_scope("episode"):
        grads, loss = episode(got_rows, got_codes, ways_ref[...], weight_ref[...])
        out_loss_ref[...] = loss

    for part in range(2):
        halves[part] = got_rows[:, part * half : (part + 1) * half]

    def term(which):
        value = dot(halves[which], grads, 0, 0)
        return jnp.concatenate(
            [value[:, i * LANES : (i + 1) * LANES] for i in range(D // LANES)], axis=0
        )

    fold_send[...] = term(1 - core).astype(BF16)
    fold = pltpu.make_async_remote_copy(
        src_ref=fold_send,
        dst_ref=fold_recv,
        send_sem=fold_ss,
        recv_sem=fold_rs,
        device_id=(twin, group),
        device_id_type=MESH,
    )
    fold.start()
    own = term(core)
    outgoing = dot(grads, weight_ref[...], 1, 1).astype(BF16)
    back_send[...] = outgoing.reshape(back_send.shape)
    back_recv[me] = back_send[me]
    with jax.named_scope("fold_wait"):
        fold.wait_recv()
    part_send[...] = (own + fold_recv[...].astype(F32)).astype(BF16).reshape(part_send.shape)

    def along(axis, source, target, send_sem, recv_sem):
        for place, peer in lines[axis][1]:
            pltpu.make_async_remote_copy(
                src_ref=source(place),
                dst_ref=target,
                send_sem=send_sem,
                recv_sem=recv_sem,
                device_id=(peer, group),
                device_id_type=MESH,
            ).start()

    def send_back(peers):
        with jax.named_scope("send_back"):
            for peer in peers:
                pltpu.make_async_remote_copy(
                    src_ref=back_send.at[peer],
                    dst_ref=back_recv.at[me],
                    send_sem=back_ss,
                    recv_sem=back_rs,
                    device_id=(peer, group),
                    device_id_type=MESH,
                ).start()

    for i in range(2):
        here = lines[i][0]
        along(i, lambda p: part_send.at[i, p], part_recv.at[i, here], part_ss.at[i], part_rs.at[i])
        part_recv[i, here] = part_send[i, here]
    send_back(row_peers[: BACK[0]])
    for i in range(2):
        with jax.named_scope(f"part_wait{i}"):
            arrived(part_recv.at[i, pl.ds(0, side - 1)], part_rs.at[i])
        line_send[i] = jnp.sum(part_recv[i].astype(F32), axis=0).astype(BF16)
        here = lines[1 - i][0]
        along(1 - i, lambda p: line_send.at[i], line_recv.at[i, here], line_ss.at[i], line_rs.at[i])
        line_recv[i, here] = line_send[i]
    send_back(row_peers[BACK[0] : BACK[1]])
    for i in range(2):
        with jax.named_scope(f"line_wait{i}"):
            arrived(line_recv.at[i, pl.ds(0, side - 1)], line_rs.at[i])
        cross_send[i] = jnp.sum(line_recv[i].astype(F32), axis=0).astype(BF16)
        for peer in groups:
            pltpu.make_async_remote_copy(
                src_ref=cross_send.at[i],
                dst_ref=cross_recv.at[i, group],
                send_sem=cross_ss.at[i],
                recv_sem=cross_rs.at[i],
                device_id=(me, peer),
                device_id_type=MESH,
            ).start()
        cross_recv[i, group] = cross_send[i]
    send_back(row_peers[BACK[1] :])
    for i in range(2):
        with jax.named_scope(f"cross_wait{i}"):
            arrived(cross_recv.at[i, pl.ds(0, n_group - 1)], cross_rs.at[i])
        here = lines[i][0]
        whole[core, i, here] = jnp.sum(cross_recv[i].astype(F32), axis=0).astype(BF16)
        final = whole.at[core, i, here]
        along(i, lambda p: final, final, whole_ss.at[i], whole_rs.at[i])

    others = back_recv.at[pl.ds(0, n - 1)]
    with jax.named_scope("back_wait"):
        pltpu.make_async_copy(others, others, back_rs).wait()
    returned = back_recv[...].reshape(n * CAP, D)
    out_rows_ref[...] = dot(hot, returned, 0, 0).astype(BF16)

    with jax.named_scope("whole_wait"):
        for i in range(2):
            arrived(whole.at[0, i, pl.ds(0, side - 1)], whole_rs.at[i])
    last = pltpu.make_async_remote_copy(
        src_ref=whole.at[core],
        dst_ref=whole.at[core],
        send_sem=twin_ss,
        recv_sem=twin_rs,
        device_id=(twin, group),
        device_id_type=MESH,
    )
    last.start()
    lay_out(whole, out_weight_ref, core)
    sent = rows_send.at[pl.ds(0, n - 1)]
    pltpu.make_async_copy(sent, sent, rows_ss).wait()
    sent = back_send.at[pl.ds(0, n - 1)]
    pltpu.make_async_copy(sent, sent, back_ss).wait()
    for i in range(2):
        arrived(part_recv.at[i, pl.ds(0, side - 1)], part_ss.at[i])
        arrived(line_recv.at[i, pl.ds(0, side - 1)], line_ss.at[i])
        arrived(cross_recv.at[i, pl.ds(0, n_group - 1)], cross_ss.at[i])
        arrived(part_recv.at[i, pl.ds(0, side - 1)], whole_ss.at[i])
    fold.wait_send()
    with jax.named_scope("last_wait"):
        last.wait()
    lay_out(whole, out_weight_ref, 1 - core)


def put_out(rows_ref, terms_ref, loss_ref, out_rows, out_terms, out_loss, sems):
    pairs = ((terms_ref, out_terms), (rows_ref, out_rows), (loss_ref, out_loss))
    copies = [pltpu.make_async_copy(a, b, sems.at[i]) for i, (a, b) in enumerate(pairs)]
    for copy in copies:
        copy.start()
    for copy in copies:
        copy.wait()


def on_device(n, n_group, features, weight, owner, slots, queries, ways):
    rows = features.shape[0]
    chips = n // 2
    lines = D * D // 2 // LANES
    vmem = pl.BlockSpec(memory_space=pltpu.VMEM)
    dma = pltpu.SemaphoreType.DMA
    side = math.isqrt(chips)
    part = (2, side, lines // (2 * side), LANES)
    hbm = pl.BlockSpec(memory_space=pl.ANY)
    own_rows, terms, losses = pl.pallas_call(
        functools.partial(kernel, n, n_group),
        out_shape=(
            pltpu.VMEM((rows, D), BF16),
            pltpu.VMEM((D, D), F32),
            pltpu.VMEM((1, 1), F32),
        ),
        in_specs=[hbm] * 6,
        out_specs=(vmem, vmem, vmem),
        scratch_shapes=[
            pltpu.VMEM((1, rows), I32),
            pltpu.VMEM((1, rows), I32),
            pltpu.VMEM((1, rows), I32),
            pltpu.VMEM((1, 1), I32),
            pltpu.VMEM((rows, D), BF16),
            pltpu.VMEM((D, D), BF16),
            pltpu.VMEM((n, CAP, D + LANES), BF16),
            pltpu.VMEM((n, CAP, D + LANES), BF16),
            pltpu.VMEM((n, CAP, D), BF16),
            pltpu.VMEM((n, CAP, D), BF16),
            pltpu.VMEM((2, n * CAP, D // 2), BF16),
            pltpu.VMEM((lines, LANES), BF16),
            pltpu.VMEM((lines, LANES), BF16),
            pltpu.VMEM(part, BF16),
            pltpu.VMEM(part, BF16),
            pltpu.VMEM((2, *part[2:]), BF16),
            pltpu.VMEM(part, BF16),
            pltpu.VMEM((2, *part[2:]), BF16),
            pltpu.VMEM((2, n_group, *part[2:]), BF16),
            pltpu.VMEM((2, *part), BF16),
            pltpu.SemaphoreType.DMA((6,)),
        ]
        + [dma] * 6
        + [pltpu.SemaphoreType.DMA((2,))] * 8
        + [dma] * 2,
        compiler_params=pltpu.CompilerParams(collective_id=0, has_side_effects=True),
        name="episodes",
    )(
        owner.reshape(1, rows),
        slots.reshape(1, rows),
        queries.reshape(1, rows),
        ways.reshape(1, 1),
        features,
        weight,
    )
    own_rows, terms, losses = pl.pallas_call(
        put_out,
        out_shape=(
            jax.ShapeDtypeStruct((rows, D), BF16),
            jax.ShapeDtypeStruct((D, D), F32),
            jax.ShapeDtypeStruct((1, 1), F32),
        ),
        in_specs=[vmem] * 3,
        out_specs=(hbm, hbm, hbm),
        scratch_shapes=[pltpu.SemaphoreType.DMA((3,))],
        name="results",
    )(*(pltpu.with_memory_space_constraint(x, pltpu.VMEM) for x in (own_rows, terms, losses)))
    return own_rows, terms, losses.reshape(1)


def solution(mesh):
    both = P(("dp", "group"))
    lines = P(("dp", "group"), None)
    return jax.shard_map(
        functools.partial(on_device, mesh.shape["dp"], mesh.shape["group"]),
        mesh=mesh,
        in_specs=(lines, P(), lines, both, both, both),
        out_specs=(lines, P(), both),
        check_vma=False,
    )
```

time: 70.1 us -> 57.6 us (0.82)
  Pallas kernels: 61.9 us -> 56.1 us
  local copies, waits for them, and re-layouts: 3.76 us -> 0 us
  between operations: 3.02 us -> 1.29 us
  other arithmetic: 1.11 us -> 0 us
    pallas_call x1 -> x2, Pallas kernels: 61.9 us -> 56.1 us  [the longest x1 54.5 us: on_device(): pl.pallas_call(functools.partial(kernel, n, n_group), out_shape=(pltpu.VM...]
    unnamed x7 -> x0, local copies, waits for them, and re-layouts: 3.09 us -> none
    convert_element_type x1 -> x0, other arithmetic: 1.11 us -> none  [on_device(): grad_weight = jnp.swapaxes(blocks, 1, 2).reshape(D, D).astype(F32)]
where the time goes in v2:
time: 57.6 us; the launch traced here: 57.4 us
  Pallas kernels  56.1 us (97%)
  between operations  1.29 us (2%)
    pallas_call x1, Pallas kernels, on_device(): pl.pallas_call(functools.partial(kernel, n, n_group), out_shape=(pltpu.VM...  54.5 us
    pallas_call x1, Pallas kernels, on_device(): pl.pallas_call(put_out, out_shape=(jax.ShapeDtypeStruct((rows, D), BF16),...  1.66 us

profile of v2, /device:TPU:1, one launch (start us, length us, event | category | flops | bytes accessed | tf_op | source)
XLA Modules:
  0.0 57.4 jit_solution(2988518113133142893)
XLA Ops:
  1.3 54.5 %episodes.1 = (bf16[128,512]{1,0:T(8,128)(2,1)S(1)}, f32[512,512]{1,0:T(8,128)S(1)}, f32[1,1]{1,0:T(1,128)}) custom-call(s32[1,128]{1,0:T(1,128)} %bitcast.6, s32[1,128]{1,0:T(1,128)} %bitcast.7, s32[1,128]{1,0:T(1,128)} %bitcast.8, s32[1,1]{1,0:T(1,128)} %bitcast.5.ways_hbm, bf16[128,512]{1,0:T(8,128)(2,1)} %features_hbm.1, bf16[512,512]{1,0:T(8,128)(2,1)} %weight_hbm.1), custom_call_target="tpu_custom_call" | custom-call | tf_op jit(solution)/shard_map/episodes/pallas_call | solution.py:389
  55.8 1.7 %results.1 = (bf16[128,512]{1,0:T(8,128)(2,1)}, f32[512,512]{1,0:T(8,128)}, f32[1,1]{1,0:T(1,128)}) custom-call(bf16[128,512]{1,0:T(8,128)(2,1)S(1)} %get-tuple-element.9.rows_ref, f32[512,512]{1,0:T(8,128)S(1)} %get-tuple-element.10.terms_ref, f32[1,1]{1,0:T(1,128)} %get-tuple-element.11.loss_ref), custom_call_target="tpu_custom_call" | custom-call | tf_op jit(solution)/shard_map/results/pallas_call | solution.py:434

commit v3 on v2

v3 whole, which is shorter than its diff:
```python
import functools
import math

import jax
import jax.numpy as jnp
from jax import lax
from jax.experimental import pallas as pl
from jax.experimental.pallas import tpu as pltpu
from jax.sharding import PartitionSpec as P

D = 512
WAYS_MAX = 50
CLASSES = 64
CAP = 2
LANES = 128
MESH = pl.DeviceIdType.MESH
F32 = jnp.float32
BF16 = jnp.bfloat16
I32 = jnp.int32
BACK = ((0, 0, 127), (0, 127, 127))


def dot(a, b, ca, cb):
    return lax.dot_general(a, b, (((ca,), (cb,)), ((), ())), preferred_element_type=F32)


def iota(shape, dim):
    return lax.broadcasted_iota(I32, shape, dim)


def three_parts(x):
    hi = x.astype(BF16)
    rest = x - hi.astype(F32)
    mid = rest.astype(BF16)
    low = (rest - mid.astype(F32)).astype(BF16)
    return hi, mid, low


def to_lanes(column):
    n = column.shape[0]
    same = iota((n, n), 0) == iota((n, n), 1)
    return jnp.sum(jnp.where(same, column, 0.0), axis=0, keepdims=True)


def to_sublanes(row):
    n = row.shape[1]
    same = iota((n, n), 0) == iota((n, n), 1)
    return jnp.sum(jnp.where(same, row, 0.0), axis=1, keepdims=True)


def episode(rows, codes, ways, weight):
    count = rows.shape[0]
    embeds = dot(rows, weight, 1, 0).astype(BF16)
    wide = embeds.astype(F32)
    code = codes.astype(I32)
    value = jnp.maximum(code - 1, 0)
    live = code > 0
    odd = lax.rem(value, 2) == 1
    query = (live & odd).astype(F32)
    label = lax.div(value, 2)
    for factor in (8, 4, 2, 1):
        label = jnp.where(label >= factor * ways, label - factor * ways, label)
    classes = iota((CLASSES, count), 0)
    hot = classes == label
    support = jnp.where(hot & live & jnp.logical_not(odd), 1.0, 0.0)
    counts = jnp.maximum(jnp.sum(support, axis=1, keepdims=True), 1.0)
    support = support.astype(BF16)
    protos = dot(support, embeds, 1, 0) / counts
    parts = three_parts(protos)
    crosses = dot(jnp.concatenate(parts, axis=0), embeds, 1, 1)
    cross = crosses[:CLASSES] + crosses[CLASSES : 2 * CLASSES] + crosses[2 * CLASSES :]
    norm_e = to_lanes(jnp.sum(wide * wide, axis=1, keepdims=True))
    norm_p = jnp.sum(protos * protos, axis=1, keepdims=True)
    distance = norm_e - 2.0 * cross + norm_p
    scores = -distance * D ** (-0.5)
    masked = jnp.where(classes < ways, scores, -1e30)
    top = jnp.max(masked, axis=0, keepdims=True)
    powers = jnp.exp(masked - top)
    total = jnp.sum(powers, axis=0, keepdims=True)
    picked = jnp.sum(jnp.where(hot, scores, 0.0), axis=0, keepdims=True)
    per_query = jnp.where(query > 0.0, top + jnp.log(total) - picked, 0.0)
    queries = jnp.maximum(jnp.sum(query, axis=1, keepdims=True), 1.0)
    loss = jnp.sum(per_query, axis=1, keepdims=True) / queries
    share = query / queries
    by_dist = (jnp.where(hot, 1.0, 0.0) - powers / total) * (share * D ** (-0.5))
    by_parts = three_parts(by_dist)
    pulls = dot(jnp.concatenate(by_parts, axis=0), embeds, 1, 0)
    pull = pulls[:CLASSES] + pulls[CLASSES : 2 * CLASSES] + pulls[2 * CLASSES :]
    by_sums = 2.0 * (protos * jnp.sum(by_dist, axis=1, keepdims=True) - pull) / counts
    sum_parts = three_parts(by_sums)
    left = jnp.concatenate([by_parts[0], by_parts[0], by_parts[1], support, support], axis=0)
    right = jnp.concatenate(
        [-2.0 * parts[0], -2.0 * parts[1], -2.0 * parts[0], sum_parts[0], sum_parts[1]], axis=0
    )
    own = to_sublanes(jnp.sum(by_dist, axis=0, keepdims=True))
    grads = dot(left, right, 0, 0) + 2.0 * own * wide
    return grads.astype(BF16), loss


def farthest_first(count):
    return sorted(range(count), key=lambda i: -min(i, count - i))


def one_hot(places, count):
    return jnp.where(iota((count, places.shape[1]), 0) == places, 1.0, 0.0).astype(BF16)


def arrived(block, sem):
    pltpu.make_async_copy(block, block, sem).wait()


def lay_out(blocks, out_ref, which):
    lines = out_ref.shape[0] // 2
    value = blocks[which].reshape(D // LANES, lines, LANES)
    start = which * lines
    for i in range(D // LANES):
        out_ref[start : start + lines, i * LANES : (i + 1) * LANES] = value[i].astype(F32)


def kernel(
    n,
    n_group,
    owner_hbm,
    slot_hbm,
    query_hbm,
    ways_hbm,
    features_hbm,
    weight_hbm,
    out_rows_ref,
    out_weight_ref,
    out_loss_ref,
    owner_ref,
    slot_ref,
    query_ref,
    ways_ref,
    features_ref,
    weight_ref,
    code_send,
    code_mid,
    code_recv,
    left_send,
    left_mid,
    left_recv,
    right_send,
    right_mid,
    right_recv,
    back_send,
    back_recv,
    halves,
    fold_send,
    fold_recv,
    part_send,
    part_recv,
    line_send,
    line_recv,
    cross_send,
    cross_recv,
    whole,
    load_sem,
    code_ss,
    code_rs,
    left_ss,
    left_rs,
    right_ss,
    right_rs,
    back_ss,
    back_rs,
    fold_ss,
    fold_rs,
    part_ss,
    part_rs,
    line_ss,
    line_rs,
    cross_ss,
    cross_rs,
    whole_ss,
    whole_rs,
    twin_ss,
    twin_rs,
    tick,
):
    me = lax.axis_index("dp")
    group = lax.axis_index("group")
    chips = n // 2
    side = math.isqrt(chips)
    core = lax.rem(me, 2)
    chip = lax.div(me, 2)
    high = lax.div(chip, side)
    low = lax.rem(chip, side)
    twin = me + 1 - 2 * core
    rows = features_ref.shape[0]
    half = D // 2
    offsets = farthest_first(side)
    highs = [lax.rem(high + i, side) * (2 * side) for i in range(side)]
    lows = [lax.rem(low + i, side) * 2 for i in range(side)]
    wide = 2 * side
    mine = 2 * low + core
    row_line = [(2 * lax.rem(low + i, side) + c, highs[0] + lows[i] + c) for i in offsets if i for c in range(2)]
    row_line.append((mine + 1 - 2 * core, twin))
    groups = [lax.rem(group + i, n_group) for i in range(1, n_group)]
    plane = [(h, w) for h in offsets for w in offsets if h or w]
    row_peers = [highs[h] + lows[w] + c for h, w in plane for c in range(2)] + [twin]
    lines = [
        (low, [(lax.rem(low + i, side), highs[0] + lows[i] + core) for i in offsets if i]),
        (high, [(lax.rem(high + i, side), highs[i] + lows[0] + core) for i in offsets if i]),
    ]

    barrier = pltpu.get_barrier_semaphore()
    with jax.named_scope("greet"):
        for _, peer in row_line + lines[1][1]:
            pl.semaphore_signal(barrier, inc=1, device_id=(peer, group), device_id_type=MESH)
        for peer in groups:
            pl.semaphore_signal(barrier, inc=1, device_id=(me, peer), device_id_type=MESH)
    loads = [
        pltpu.make_async_copy(source, target, load_sem.at[i])
        for i, (source, target) in enumerate(
            (
                (owner_hbm, owner_ref),
                (features_hbm, features_ref),
                (slot_hbm, slot_ref),
                (query_hbm, query_ref),
                (ways_hbm, ways_ref),
                (weight_hbm, weight_ref),
            )
        )
    ]
    for load in loads:
        load.start()
    for load in loads:
        load.wait()

    owner_lane = owner_ref[...].astype(F32)
    owner = to_sublanes(owner_lane)
    earlier = (owner == owner_lane) & (iota((rows, rows), 0) < iota((rows, rows), 1))
    place = jnp.sum(jnp.where(earlier, 1.0, 0.0), axis=0, keepdims=True)
    codes = (slot_ref[...] * 2 + query_ref[...] + 1).astype(F32)
    weighed = to_sublanes(codes * jnp.where(place > 0.0, 1.0 * LANES, 1.0))
    code_send[...] = jnp.sum(
        jnp.where(owner == iota((rows, n), 1).astype(F32), weighed, 0.0), axis=0, keepdims=True
    )
    code_mid[mine] = code_send[...]
    target = owner_lane.astype(I32)
    place = place.astype(I32)
    hot = one_hot(target * CAP + place, n * CAP)
    turned = (lax.rem(target, wide) * side + lax.div(target, wide)) * CAP + place
    left = dot(one_hot(turned, n * CAP), features_ref[:, :half], 1, 0).astype(BF16)
    left_send[...] = left.reshape(left_send.shape)
    right = dot(hot, features_ref[:, half:], 1, 0).astype(BF16)
    right_send[...] = right.reshape(right_send.shape)
    left_mid[:, mine] = left_send[mine]
    right_mid[:, high] = right_send[high]

    with jax.named_scope("barrier_wait"):
        pl.semaphore_wait(barrier, wide + side + n_group - 3)

    def push(source, target, send_sem, recv_sem, peer):
        pltpu.make_async_remote_copy(
            src_ref=source,
            dst_ref=target,
            send_sem=send_sem,
            recv_sem=recv_sem,
            device_id=(peer, group),
            device_id_type=MESH,
        ).start()

    with jax.named_scope("send_rows"):
        for place, peer in row_line:
            push(code_send, code_mid.at[mine], code_ss.at[0], code_rs.at[0], peer)
        for place, peer in row_line:
            push(left_send.at[place], left_mid.at[:, mine], left_ss.at[0], left_rs.at[0], peer)
        for place, peer in lines[1][1]:
            push(right_send.at[place], right_mid.at[:, high], right_ss.at[0], right_rs.at[0], peer)
    with jax.named_scope("code_wait0"):
        arrived(code_mid.at[pl.ds(0, wide - 1)], code_rs.at[0])
    for place, peer in lines[1][1]:
        push(code_mid, code_recv.at[high], code_ss.at[1], code_rs.at[1], peer)
    code_recv[high] = code_mid[...]
    with jax.named_scope("left_wait0"):
        arrived(left_mid.at[:, pl.ds(0, wide - 1)], left_rs.at[0])
    for place, peer in lines[1][1]:
        push(left_mid.at[place], left_recv.at[high], left_ss.at[1], left_rs.at[1], peer)
    left_recv[high] = left_mid[high]
    with jax.named_scope("right_wait0"):
        arrived(right_mid.at[:, pl.ds(0, side - 1)], right_rs.at[0])
    for place, peer in row_line:
        push(right_mid.at[place], right_recv.at[:, mine], right_ss.at[1], right_rs.at[1], peer)
    right_recv[:, mine] = right_mid[mine]
    with jax.named_scope("code_wait1"):
        arrived(code_recv.at[pl.ds(0, side - 1)], code_rs.at[1])
    table = code_recv[...].reshape(n, n)
    both = jnp.sum(jnp.where(iota((n, n), 1) == me, table, 0.0), axis=1, keepdims=True).astype(I32)
    spot = iota((n, n * CAP), 1)
    chosen = jnp.where(lax.rem(spot, CAP) == 0, lax.rem(both, LANES), lax.div(both, LANES))
    chosen = jnp.where(lax.div(spot, CAP) == iota((n, n * CAP), 0), chosen, 0)
    got_codes = jnp.sum(chosen.astype(F32), axis=0, keepdims=True)
    with jax.named_scope("left_wait1"):
        arrived(left_recv.at[pl.ds(0, side - 1)], left_rs.at[1])
    halves[0] = left_recv[...].reshape(n * CAP, half)
    with jax.named_scope("right_wait1"):
        arrived(right_recv.at[:, pl.ds(0, wide - 1)], right_rs.at[1])
    halves[1] = right_recv[...].reshape(n * CAP, half)
    got_rows = jnp.concatenate([halves[0], halves[1]], axis=1)
    with jax.named_scope("episode"):
        grads, loss = episode(got_rows, got_codes, ways_ref[...], weight_ref[...])
        out_loss_ref[...] = loss

    def term(which):
        value = dot(halves[which], grads, 0, 0)
        return jnp.concatenate(
            [value[:, i * LANES : (i + 1) * LANES] for i in range(D // LANES)], axis=0
        )

    def fold(which):
        return pltpu.make_async_remote_copy(
            src_ref=fold_send.at[which],
            dst_ref=fold_recv.at[which],
            send_sem=fold_ss.at[which],
            recv_sem=fold_rs.at[which],
            device_id=(twin, group),
            device_id_type=MESH,
        )

    def last(which):
        return pltpu.make_async_remote_copy(
            src_ref=whole.at[which],
            dst_ref=whole.at[which],
            send_sem=twin_ss.at[which],
            recv_sem=twin_rs.at[which],
            device_id=(twin, group),
            device_id_type=MESH,
        )

    def prepare_back():
        outgoing = dot(grads, weight_ref[...], 1, 1).astype(BF16)
        back_send[...] = outgoing.reshape(back_send.shape)
        back_recv[me] = back_send[me]

    def send_back(which, piece):
        with jax.named_scope(f"send_back{piece}"):
            for peer in row_peers[BACK[which][piece] : BACK[which][piece + 1]]:
                push(back_send.at[peer], back_recv.at[me], back_ss, back_rs, peer)

    def take_back():
        with jax.named_scope("back_wait"):
            arrived(back_recv.at[pl.ds(0, n - 1)], back_rs)
        returned = back_recv[...].reshape(n * CAP, D)
        out_rows_ref[...] = dot(hot, returned, 0, 0).astype(BF16)

    def spread(axis, source, target, send_sem, recv_sem):
        for place, peer in lines[axis][1]:
            push(source(place), target, send_sem, recv_sem, peer)

    def tell():
        pl.semaphore_signal(tick, inc=1, device_id=(twin, group), device_id_type=MESH)

    @pl.when(core == 1)
    def _():
        own = [term(0), term(1)]
        prepare_back()
        for i in range(2):
            with jax.named_scope(f"fold_wait{i}"):
                fold(i).wait_recv()
            total = own[i] + fold_recv[i].astype(F32)
            part_send[i] = total.astype(BF16).reshape(part_send.shape[1:])
            here = lines[i][0]
            spread(i, lambda p: part_send.at[i, p], part_recv.at[i, here], part_ss.at[i], part_rs.at[i])
            part_recv[i, here] = part_send[i, here]
        for i in range(2):
            with jax.named_scope(f"part_wait{i}"):
                arrived(part_recv.at[i, pl.ds(0, side - 1)], part_rs.at[i])
            line_send[i] = jnp.sum(part_recv[i].astype(F32), axis=0).astype(BF16)
            here = lines[1 - i][0]
            spread(1 - i, lambda p: line_send.at[i], line_recv.at[i, here], line_ss.at[i], line_rs.at[i])
            line_recv[i, here] = line_send[i]
        tell()
        send_back(1, 0)
        for i in range(2):
            with jax.named_scope(f"line_wait{i}"):
                arrived(line_recv.at[i, pl.ds(0, side - 1)], line_rs.at[i])
            cross_send[i] = jnp.sum(line_recv[i].astype(F32), axis=0).astype(BF16)
            for peer in groups:
                pltpu.make_async_remote_copy(
                    src_ref=cross_send.at[i],
                    dst_ref=cross_recv.at[i, group],
                    send_sem=cross_ss.at[i],
                    recv_sem=cross_rs.at[i],
                    device_id=(me, peer),
                    device_id_type=MESH,
                ).start()
            cross_recv[i, group] = cross_send[i]
        tell()
        send_back(1, 1)
        for i in range(2):
            with jax.named_scope(f"cross_wait{i}"):
                arrived(cross_recv.at[i, pl.ds(0, n_group - 1)], cross_rs.at[i])
            here = lines[i][0]
            whole[i, here] = jnp.sum(cross_recv[i].astype(F32), axis=0).astype(BF16)
            final = whole.at[i, here]
            spread(i, lambda p: final, final, whole_ss.at[i], whole_rs.at[i])
        for i in range(2):
            with jax.named_scope(f"whole_wait{i}"):
                arrived(whole.at[i, pl.ds(0, side - 1)], whole_rs.at[i])
            last(i).start()
        for i in range(2):
            lay_out(whole, out_weight_ref, i)
        take_back()
        for i in range(2):
            arrived(part_recv.at[i, pl.ds(0, side - 1)], part_ss.at[i])
            arrived(line_recv.at[i, pl.ds(0, side - 1)], line_ss.at[i])
            arrived(cross_recv.at[i, pl.ds(0, n_group - 1)], cross_ss.at[i])
            arrived(part_recv.at[i, pl.ds(0, side - 1)], whole_ss.at[i])
            last(i).wait_send()

    @pl.when(core == 0)
    def _():
        for i in range(2):
            fold_send[i] = term(i).astype(BF16)
            fold(i).start()
        prepare_back()
        for piece in range(2):
            with jax.named_scope(f"tick_wait{piece}"):
                pl.semaphore_wait(tick, 1)
            send_back(0, piece)
        take_back()
        for i in range(2):
            fold(i).wait_send()
            with jax.named_scope(f"last_wait{i}"):
                last(i).wait_recv()
            lay_out(whole, out_weight_ref, i)

    arrived(code_mid.at[pl.ds(0, wide - 1)], code_ss.at[0])
    arrived(code_recv.at[pl.ds(0, side - 1)], code_ss.at[1])
    arrived(left_mid.at[:, pl.ds(0, wide - 1)], left_ss.at[0])
    arrived(left_recv.at[pl.ds(0, side - 1)], left_ss.at[1])
    arrived(right_mid.at[:, pl.ds(0, side - 1)], right_ss.at[0])
    arrived(right_recv.at[:, pl.ds(0, wide - 1)], right_ss.at[1])
    arrived(back_send.at[pl.ds(0, n - 1)], back_ss)


def put_out(rows_ref, terms_ref, loss_ref, out_rows, out_terms, out_loss, sems):
    pairs = ((terms_ref, out_terms), (rows_ref, out_rows), (loss_ref, out_loss))
    copies = [pltpu.make_async_copy(a, b, sems.at[i]) for i, (a, b) in enumerate(pairs)]
    for copy in copies:
        copy.start()
    for copy in copies:
        copy.wait()


def on_device(n, n_group, features, weight, owner, slots, queries, ways):
    rows = features.shape[0]
    chips = n // 2
    lines = D * D // LANES
    vmem = pl.BlockSpec(memory_space=pltpu.VMEM)
    dma = pltpu.SemaphoreType.DMA
    side = math.isqrt(chips)
    part = (2, side, lines // (2 * side), LANES)
    hbm = pl.BlockSpec(memory_space=pl.ANY)
    own_rows, terms, losses = pl.pallas_call(
        functools.partial(kernel, n, n_group),
        out_shape=(
            pltpu.VMEM((rows, D), BF16),
            pltpu.VMEM((D, D), F32),
            pltpu.VMEM((1, 1), F32),
        ),
        in_specs=[hbm] * 6,
        out_specs=(vmem, vmem, vmem),
        scratch_shapes=[
            pltpu.VMEM((1, rows), I32),
            pltpu.VMEM((1, rows), I32),
            pltpu.VMEM((1, rows), I32),
            pltpu.VMEM((1, 1), I32),
            pltpu.VMEM((rows, D), BF16),
            pltpu.VMEM((D, D), BF16),
            pltpu.VMEM((1, n), F32),
            pltpu.VMEM((2 * side, 1, n), F32),
            pltpu.VMEM((side, 2 * side, 1, n), F32),
            pltpu.VMEM((2 * side, side, CAP, D // 2), BF16),
            pltpu.VMEM((side, 2 * side, CAP, D // 2), BF16),
            pltpu.VMEM((side, 2 * side, CAP, D // 2), BF16),
            pltpu.VMEM((side, 2 * side, CAP, D // 2), BF16),
            pltpu.VMEM((2 * side, side, CAP, D // 2), BF16),
            pltpu.VMEM((side, 2 * side, CAP, D // 2), BF16),
            pltpu.VMEM((n, CAP, D), BF16),
            pltpu.VMEM((n, CAP, D), BF16),
            pltpu.VMEM((2, n * CAP, D // 2), BF16),
            pltpu.VMEM((2, lines // 2, LANES), BF16),
            pltpu.VMEM((2, lines // 2, LANES), BF16),
            pltpu.VMEM(part, BF16),
            pltpu.VMEM(part, BF16),
            pltpu.VMEM((2, *part[2:]), BF16),
            pltpu.VMEM(part, BF16),
            pltpu.VMEM((2, *part[2:]), BF16),
            pltpu.VMEM((2, n_group, *part[2:]), BF16),
            pltpu.VMEM(part, BF16),
            pltpu.SemaphoreType.DMA((6,)),
        ]
        + [pltpu.SemaphoreType.DMA((2,))] * 6
        + [dma] * 2
        + [pltpu.SemaphoreType.DMA((2,))] * 12
        + [pltpu.SemaphoreType.REGULAR],
        compiler_params=pltpu.CompilerParams(collective_id=0, has_side_effects=True),
        name="episodes",
    )(
        owner.reshape(1, rows),
        slots.reshape(1, rows),
        queries.reshape(1, rows),
        ways.reshape(1, 1),
        features,
        weight,
    )
    own_rows, terms, losses = pl.pallas_call(
        put_out,
        out_shape=(
            jax.ShapeDtypeStruct((rows, D), BF16),
            jax.ShapeDtypeStruct((D, D), F32),
            jax.ShapeDtypeStruct((1, 1), F32),
        ),
        in_specs=[vmem] * 3,
        out_specs=(hbm, hbm, hbm),
        scratch_shapes=[pltpu.SemaphoreType.DMA((3,))],
        name="results",
    )(*(pltpu.with_memory_space_constraint(x, pltpu.VMEM) for x in (own_rows, terms, losses)))
    return own_rows, terms, losses.reshape(1)


def solution(mesh):
    both = P(("dp", "group"))
    lines = P(("dp", "group"), None)
    return jax.shard_map(
        functools.partial(on_device, mesh.shape["dp"], mesh.shape["group"]),
        mesh=mesh,
        in_specs=(lines, P(), lines, both, both, both),
        out_specs=(lines, P(), both),
        check_vma=False,
    )
```

time: 57.6 us -> 56 us (0.972)
  Pallas kernels: 56.1 us -> 54.5 us
    pallas_call x1, Pallas kernels: 54.5 us -> 52.8 us  [on_device(): pl.pallas_call(functools.partial(kernel, n, n_group), out_shape=(pltpu.VM...]
where the time goes in v3:
time: 56 us; the launch traced here: 55.8 us
  Pallas kernels  54.5 us (97%)
  between operations  1.29 us (2%)
    pallas_call x1, Pallas kernels, on_device(): pl.pallas_call(functools.partial(kernel, n, n_group), out_shape=(pltpu.VM...  52.8 us
    pallas_call x1, Pallas kernels, on_device(): pl.pallas_call(put_out, out_shape=(jax.ShapeDtypeStruct((rows, D), BF16),...  1.66 us

profile of v3, /device:TPU:1, one launch (start us, length us, event | category | flops | bytes accessed | tf_op | source)
XLA Modules:
  0.0 55.8 jit_solution(2531375097857413557)
XLA Ops:
  1.3 52.8 %episodes.1 = (bf16[128,512]{1,0:T(8,128)(2,1)S(1)}, f32[512,512]{1,0:T(8,128)S(1)}, f32[1,1]{1,0:T(1,128)}) custom-call(s32[1,128]{1,0:T(1,128)} %bitcast.6, s32[1,128]{1,0:T(1,128)} %bitcast.7, s32[1,128]{1,0:T(1,128)} %bitcast.8, s32[1,1]{1,0:T(1,128)} %bitcast.5.ways_hbm, bf16[128,512]{1,0:T(8,128)(2,1)} %features_hbm.1, bf16[512,512]{1,0:T(8,128)(2,1)} %weight_hbm.1), custom_call_target="tpu_custom_call" | custom-call | tf_op jit(solution)/shard_map/episodes/pallas_call | solution.py:458
  54.1 1.7 %results.1 = (bf16[128,512]{1,0:T(8,128)(2,1)}, f32[512,512]{1,0:T(8,128)}, f32[1,1]{1,0:T(1,128)}) custom-call(bf16[128,512]{1,0:T(8,128)(2,1)S(1)} %get-tuple-element.9.rows_ref, f32[512,512]{1,0:T(8,128)S(1)} %get-tuple-element.10.terms_ref, f32[1,1]{1,0:T(1,128)} %get-tuple-element.11.loss_ref), custom_call_target="tpu_custom_call" | custom-call | tf_op jit(solution)/shard_map/results/pallas_call | solution.py:511

commit v4 on v3

--- a/solution.py
+++ b/solution.py
@@ -17,7 +17,8 @@
 F32 = jnp.float32
 BF16 = jnp.bfloat16
 I32 = jnp.int32
-BACK = ((0, 0, 127), (0, 127, 127))
+BACK = ((0, 0, 64, 127), (0, 127, 127))
+WAIT = (0, 2500)
 
 
 def dot(a, b, ca, cb):
@@ -165,8 +166,8 @@
     right_rs,
     back_ss,
     back_rs,
-    fold_ss,
-    fold_rs,
+    pair_ss,
+    pair_rs,
     part_ss,
     part_rs,
     line_ss,
@@ -175,8 +176,6 @@
     cross_rs,
     whole_ss,
     whole_rs,
-    twin_ss,
-    twin_rs,
     tick,
 ):
     me = lax.axis_index("dp")
@@ -211,22 +210,19 @@
             pl.semaphore_signal(barrier, inc=1, device_id=(peer, group), device_id_type=MESH)
         for peer in groups:
             pl.semaphore_signal(barrier, inc=1, device_id=(me, peer), device_id_type=MESH)
-    loads = [
-        pltpu.make_async_copy(source, target, load_sem.at[i])
-        for i, (source, target) in enumerate(
-            (
-                (owner_hbm, owner_ref),
-                (features_hbm, features_ref),
-                (slot_hbm, slot_ref),
-                (query_hbm, query_ref),
-                (ways_hbm, ways_ref),
-                (weight_hbm, weight_ref),
-            )
-        )
-    ]
+    pairs = (
+        (owner_hbm, owner_ref, 0),
+        (slot_hbm, slot_ref, 0),
+        (query_hbm, query_ref, 0),
+        (features_hbm, features_ref, 1),
+        (ways_hbm, ways_ref, 2),
+        (weight_hbm, weight_ref, 3),
+    )
+    loads = [pltpu.make_async_copy(source, target, load_sem.at[i]) for source, target, i in pairs]
     for load in loads:
         load.start()
-    for load in loads:
+    arrived(code_mid.at[pl.ds(0, 3)], load_sem.at[0])
+    for load in loads[3:]:
         load.wait()
 
     owner_lane = owner_ref[...].astype(F32)
@@ -265,28 +261,28 @@
 
     with jax.named_scope("send_rows"):
         for place, peer in row_line:
-            push(code_send, code_mid.at[mine], code_ss.at[0], code_rs.at[0], peer)
+            push(code_send, code_mid.at[mine], code_ss, code_rs.at[0], peer)
         for place, peer in row_line:
-            push(left_send.at[place], left_mid.at[:, mine], left_ss.at[0], left_rs.at[0], peer)
+            push(left_send.at[place], left_mid.at[:, mine], left_ss, left_rs.at[0], peer)
         for place, peer in lines[1][1]:
-            push(right_send.at[place], right_mid.at[:, high], right_ss.at[0], right_rs.at[0], peer)
+            push(right_send.at[place], right_mid.at[:, high], right_ss, right_rs.at[0], peer)
     with jax.named_scope("code_wait0"):
         arrived(code_mid.at[pl.ds(0, wide - 1)], code_rs.at[0])
     for place, peer in lines[1][1]:
-        push(code_mid, code_recv.at[high], code_ss.at[1], code_rs.at[1], peer)
-    code_recv[high] = code_mid[...]
+        push(code_mid, code_recv.at[pl.ds(high * wide, wide)], code_ss, code_rs.at[1], peer)
+    code_recv[pl.ds(high * wide, wide)] = code_mid[...]
     with jax.named_scope("left_wait0"):
         arrived(left_mid.at[:, pl.ds(0, wide - 1)], left_rs.at[0])
     for place, peer in lines[1][1]:
-        push(left_mid.at[place], left_recv.at[high], left_ss.at[1], left_rs.at[1], peer)
+        push(left_mid.at[place], left_recv.at[high], left_ss, left_rs.at[1], peer)
     left_recv[high] = left_mid[high]
     with jax.named_scope("right_wait0"):
         arrived(right_mid.at[:, pl.ds(0, side - 1)], right_rs.at[0])
     for place, peer in row_line:
-        push(right_mid.at[place], right_recv.at[:, mine], right_ss.at[1], right_rs.at[1], peer)
+        push(right_mid.at[place], right_recv.at[:, mine], right_ss, right_rs.at[1], peer)
     right_recv[:, mine] = right_mid[mine]
     with jax.named_scope("code_wait1"):
-        arrived(code_recv.at[pl.ds(0, side - 1)], code_rs.at[1])
+        arrived(code_recv.at[pl.ds(0, n - wide)], code_rs.at[1])
     table = code_recv[...].reshape(n, n)
     both = jnp.sum(jnp.where(iota((n, n), 1) == me, table, 0.0), axis=1, keepdims=True).astype(I32)
     spot = iota((n, n * CAP), 1)
@@ -314,8 +310,8 @@
         return pltpu.make_async_remote_copy(
             src_ref=fold_send.at[which],
             dst_ref=fold_recv.at[which],
-            send_sem=fold_ss.at[which],
-            recv_sem=fold_rs.at[which],
+            send_sem=pair_ss,
+            recv_sem=pair_rs.at[which],
             device_id=(twin, group),
             device_id_type=MESH,
         )
@@ -324,8 +320,8 @@
         return pltpu.make_async_remote_copy(
             src_ref=whole.at[which],
             dst_ref=whole.at[which],
-            send_sem=twin_ss.at[which],
-            recv_sem=twin_rs.at[which],
+            send_sem=pair_ss,
+            recv_sem=pair_rs.at[which],
             device_id=(twin, group),
             device_id_type=MESH,
         )
@@ -363,14 +359,14 @@
             total = own[i] + fold_recv[i].astype(F32)
             part_send[i] = total.astype(BF16).reshape(part_send.shape[1:])
             here = lines[i][0]
-            spread(i, lambda p: part_send.at[i, p], part_recv.at[i, here], part_ss.at[i], part_rs.at[i])
+            spread(i, lambda p: part_send.at[i, p], part_recv.at[i, here], part_ss, part_rs.at[i])
             part_recv[i, here] = part_send[i, here]
         for i in range(2):
             with jax.named_scope(f"part_wait{i}"):
                 arrived(part_recv.at[i, pl.ds(0, side - 1)], part_rs.at[i])
             line_send[i] = jnp.sum(part_recv[i].astype(F32), axis=0).astype(BF16)
             here = lines[1 - i][0]
-            spread(1 - i, lambda p: line_send.at[i], line_recv.at[i, here], line_ss.at[i], line_rs.at[i])
+            spread(1 - i, lambda p: line_send.at[i], line_recv.at[i, here], line_ss, line_rs.at[i])
             line_recv[i, here] = line_send[i]
         tell()
         send_back(1, 0)
@@ -382,7 +378,7 @@
                 pltpu.make_async_remote_copy(
                     src_ref=cross_send.at[i],
                     dst_ref=cross_recv.at[i, group],
-                    send_sem=cross_ss.at[i],
+                    send_sem=cross_ss,
                     recv_sem=cross_rs.at[i],
                     device_id=(me, peer),
                     device_id_type=MESH,
@@ -396,7 +392,7 @@
             here = lines[i][0]
             whole[i, here] = jnp.sum(cross_recv[i].astype(F32), axis=0).astype(BF16)
             final = whole.at[i, here]
-            spread(i, lambda p: final, final, whole_ss.at[i], whole_rs.at[i])
+            spread(i, lambda p: final, final, whole_ss, whole_rs.at[i])
         for i in range(2):
             with jax.named_scope(f"whole_wait{i}"):
                 arrived(whole.at[i, pl.ds(0, side - 1)], whole_rs.at[i])
@@ -404,12 +400,11 @@
         for i in range(2):
             lay_out(whole, out_weight_ref, i)
         take_back()
-        for i in range(2):
-            arrived(part_recv.at[i, pl.ds(0, side - 1)], part_ss.at[i])
-            arrived(line_recv.at[i, pl.ds(0, side - 1)], line_ss.at[i])
-            arrived(cross_recv.at[i, pl.ds(0, n_group - 1)], cross_ss.at[i])
-            arrived(part_recv.at[i, pl.ds(0, side - 1)], whole_ss.at[i])
-            last(i).wait_send()
+        arrived(part_recv.at[:, pl.ds(0, side - 1)], part_ss)
+        arrived(line_recv.at[:, pl.ds(0, side - 1)], line_ss)
+        arrived(cross_recv.at[:, pl.ds(0, n_group - 1)], cross_ss)
+        arrived(whole.at[:, pl.ds(0, side - 1)], whole_ss)
+        arrived(whole, pair_ss)
 
     @pl.when(core == 0)
     def _():
@@ -417,32 +412,45 @@
             fold_send[i] = term(i).astype(BF16)
             fold(i).start()
         prepare_back()
-        for piece in range(2):
-            with jax.named_scope(f"tick_wait{piece}"):
-                pl.semaphore_wait(tick, 1)
-            send_back(0, piece)
+        if WAIT[0]:
+            pl.delay(WAIT[0])
+        send_back(0, 0)
+        with jax.named_scope("tick_wait0"):
+            pl.semaphore_wait(tick, 1)
+        if WAIT[1]:
+            pl.delay(WAIT[1])
+        send_back(0, 1)
+        with jax.named_scope("tick_wait1"):
+            pl.semaphore_wait(tick, 1)
+        send_back(0, 2)
         take_back()
         for i in range(2):
-            fold(i).wait_send()
             with jax.named_scope(f"last_wait{i}"):
                 last(i).wait_recv()
             lay_out(whole, out_weight_ref, i)
-
-    arrived(code_mid.at[pl.ds(0, wide - 1)], code_ss.at[0])
-    arrived(code_recv.at[pl.ds(0, side - 1)], code_ss.at[1])
-    arrived(left_mid.at[:, pl.ds(0, wide - 1)], left_ss.at[0])
-    arrived(left_recv.at[pl.ds(0, side - 1)], left_ss.at[1])
-    arrived(right_mid.at[:, pl.ds(0, side - 1)], right_ss.at[0])
-    arrived(right_recv.at[:, pl.ds(0, wide - 1)], right_ss.at[1])
+        arrived(fold_send, pair_ss)
+
+    arrived(code_recv.at[pl.ds(0, n - 1)], code_ss)
+    sent = ((wide - 1) * side + (side - 1) * wide) // 2
+    arrived(back_send.at[pl.ds(0, sent)], left_ss)
+    arrived(back_send.at[pl.ds(0, sent)], right_ss)
     arrived(back_send.at[pl.ds(0, n - 1)], back_ss)
 
 
 def put_out(rows_ref, terms_ref, loss_ref, out_rows, out_terms, out_loss, sems):
-    pairs = ((terms_ref, out_terms), (rows_ref, out_rows), (loss_ref, out_loss))
-    copies = [pltpu.make_async_copy(a, b, sems.at[i]) for i, (a, b) in enumerate(pairs)]
-    for copy in copies:
+    pieces = 8
+    lines = terms_ref.shape[0] // pieces
+    for i in range(pieces):
+        block = pl.ds(i * lines, lines)
+        pltpu.make_async_copy(terms_ref.at[block], out_terms.at[block], sems.at[0]).start()
+    others = [
+        pltpu.make_async_copy(rows_ref, out_rows, sems.at[1]),
+        pltpu.make_async_copy(loss_ref, out_loss, sems.at[2]),
+    ]
+    for copy in others:
         copy.start()
-    for copy in copies:
+    arrived(terms_ref, sems.at[0])
+    for copy in others:
         copy.wait()
 
 
@@ -452,6 +460,7 @@
     lines = D * D // LANES
     vmem = pl.BlockSpec(memory_space=pltpu.VMEM)
     dma = pltpu.SemaphoreType.DMA
+    two = pltpu.SemaphoreType.DMA((2,))
     side = math.isqrt(chips)
     part = (2, side, lines // (2 * side), LANES)
     hbm = pl.BlockSpec(memory_space=pl.ANY)
@@ -473,7 +482,7 @@
             pltpu.VMEM((D, D), BF16),
             pltpu.VMEM((1, n), F32),
             pltpu.VMEM((2 * side, 1, n), F32),
-            pltpu.VMEM((side, 2 * side, 1, n), F32),
+            pltpu.VMEM((n, 1, n), F32),
             pltpu.VMEM((2 * side, side, CAP, D // 2), BF16),
             pltpu.VMEM((side, 2 * side, CAP, D // 2), BF16),
             pltpu.VMEM((side, 2 * side, CAP, D // 2), BF16),
@@ -492,11 +501,11 @@
             pltpu.VMEM((2, *part[2:]), BF16),
             pltpu.VMEM((2, n_group, *part[2:]), BF16),
             pltpu.VMEM(part, BF16),
-            pltpu.SemaphoreType.DMA((6,)),
+            pltpu.SemaphoreType.DMA((4,)),
         ]
-        + [pltpu.SemaphoreType.DMA((2,))] * 6
-        + [dma] * 2
-        + [pltpu.SemaphoreType.DMA((2,))] * 12
+        + [dma, two] * 3
+        + [dma, dma]
+        + [dma, two] * 5
         + [pltpu.SemaphoreType.REGULAR],
         compiler_params=pltpu.CompilerParams(collective_id=0, has_side_effects=True),
         name="episodes",

time: 56 us -> 55.5 us (level)
  no operation moved by 1% of the time
where the time goes in v4:
time: 55.5 us; the launch traced here: 55.3 us
  Pallas kernels  54 us (97%)
  between operations  1.29 us (2%)
    pallas_call x1, Pallas kernels, on_device(): pl.pallas_call(functools.partial(kernel, n, n_group), out_shape=(pltpu.VM...  52.4 us
    pallas_call x1, Pallas kernels, on_device(): pl.pallas_call(put_out, out_shape=(jax.ShapeDtypeStruct((rows, D), BF16),...  1.66 us

profile of v4, /device:TPU:1, one launch (start us, length us, event | category | flops | bytes accessed | tf_op | source)
XLA Modules:
  0.0 55.3 jit_solution(1675858362236296098)
XLA Ops:
  1.3 52.4 %episodes.1 = (bf16[128,512]{1,0:T(8,128)(2,1)S(1)}, f32[512,512]{1,0:T(8,128)S(1)}, f32[1,1]{1,0:T(1,128)}) custom-call(s32[1,128]{1,0:T(1,128)} %bitcast.6, s32[1,128]{1,0:T(1,128)} %bitcast.7, s32[1,128]{1,0:T(1,128)} %bitcast.8, s32[1,1]{1,0:T(1,128)} %bitcast.5.ways_hbm, bf16[128,512]{1,0:T(8,128)(2,1)} %features_hbm.1, bf16[512,512]{1,0:T(8,128)(2,1)} %weight_hbm.1), custom_call_target="tpu_custom_call" | custom-call | tf_op jit(solution)/shard_map/episodes/pallas_call | solution.py:467
  53.7 1.7 %results.1 = (bf16[128,512]{1,0:T(8,128)(2,1)}, f32[512,512]{1,0:T(8,128)}, f32[1,1]{1,0:T(1,128)}) custom-call(bf16[128,512]{1,0:T(8,128)(2,1)S(1)} %get-tuple-element.9.rows_ref, f32[512,512]{1,0:T(8,128)S(1)} %get-tuple-element.10.terms_ref, f32[1,1]{1,0:T(1,128)} %get-tuple-element.11.loss_ref), custom_call_target="tpu_custom_call" | custom-call | tf_op jit(solution)/shard_map/results/pallas_call | solution.py:520

commit v5 on v4

--- a/solution.py
+++ b/solution.py
@@ -17,8 +17,8 @@
 F32 = jnp.float32
 BF16 = jnp.bfloat16
 I32 = jnp.int32
-BACK = ((0, 0, 64, 127), (0, 127, 127))
-WAIT = (0, 2500)
+BACK = ((0, 127, 127), (0, 127))
+WAIT = (4000, 0)
 
 
 def dot(a, b, ca, cb):
@@ -154,8 +154,6 @@
     part_recv,
     line_send,
     line_recv,
-    cross_send,
-    cross_recv,
     whole,
     load_sem,
     code_ss,
@@ -172,8 +170,6 @@
     part_rs,
     line_ss,
     line_rs,
-    cross_ss,
-    cross_rs,
     whole_ss,
     whole_rs,
     tick,
@@ -182,6 +178,7 @@
     group = lax.axis_index("group")
     chips = n // 2
     side = math.isqrt(chips)
+    spots = side * n_group
     core = lax.rem(me, 2)
     chip = lax.div(me, 2)
     high = lax.div(chip, side)
@@ -343,8 +340,16 @@
         out_rows_ref[...] = dot(hot, returned, 0, 0).astype(BF16)
 
     def spread(axis, source, target, send_sem, recv_sem):
-        for place, peer in lines[axis][1]:
-            push(source(place), target, send_sem, recv_sem, peer)
+        for place, peer in lines[axis][1] + [(lines[axis][0], me)]:
+            for other in groups + [group] * (peer is not me):
+                pltpu.make_async_remote_copy(
+                    src_ref=source(place, other),
+                    dst_ref=target,
+                    send_sem=send_sem,
+                    recv_sem=recv_sem,
+                    device_id=(peer, other),
+                    device_id_type=MESH,
+                ).start()
 
     def tell():
         pl.semaphore_signal(tick, inc=1, device_id=(twin, group), device_id_type=MESH)
@@ -358,52 +363,36 @@
                 fold(i).wait_recv()
             total = own[i] + fold_recv[i].astype(F32)
             part_send[i] = total.astype(BF16).reshape(part_send.shape[1:])
-            here = lines[i][0]
-            spread(i, lambda p: part_send.at[i, p], part_recv.at[i, here], part_ss, part_rs.at[i])
+            here = lines[i][0] * n_group + group
+            spread(i, lambda p, g: part_send.at[i, p * n_group + g], part_recv.at[i, here], part_ss, part_rs.at[i])
             part_recv[i, here] = part_send[i, here]
         for i in range(2):
             with jax.named_scope(f"part_wait{i}"):
-                arrived(part_recv.at[i, pl.ds(0, side - 1)], part_rs.at[i])
+                arrived(part_recv.at[i, pl.ds(0, spots - 1)], part_rs.at[i])
             line_send[i] = jnp.sum(part_recv[i].astype(F32), axis=0).astype(BF16)
             here = lines[1 - i][0]
-            spread(1 - i, lambda p: line_send.at[i], line_recv.at[i, here], line_ss, line_rs.at[i])
+            for _, peer in lines[1 - i][1]:
+                push(line_send.at[i], line_recv.at[i, here], line_ss, line_rs.at[i], peer)
             line_recv[i, here] = line_send[i]
         tell()
         send_back(1, 0)
         for i in range(2):
             with jax.named_scope(f"line_wait{i}"):
                 arrived(line_recv.at[i, pl.ds(0, side - 1)], line_rs.at[i])
-            cross_send[i] = jnp.sum(line_recv[i].astype(F32), axis=0).astype(BF16)
-            for peer in groups:
-                pltpu.make_async_remote_copy(
-                    src_ref=cross_send.at[i],
-                    dst_ref=cross_recv.at[i, group],
-                    send_sem=cross_ss,
-                    recv_sem=cross_rs.at[i],
-                    device_id=(me, peer),
-                    device_id_type=MESH,
-                ).start()
-            cross_recv[i, group] = cross_send[i]
-        tell()
-        send_back(1, 1)
-        for i in range(2):
-            with jax.named_scope(f"cross_wait{i}"):
-                arrived(cross_recv.at[i, pl.ds(0, n_group - 1)], cross_rs.at[i])
-            here = lines[i][0]
-            whole[i, here] = jnp.sum(cross_recv[i].astype(F32), axis=0).astype(BF16)
+            here = lines[i][0] * n_group + group
+            whole[i, here] = jnp.sum(line_recv[i].astype(F32), axis=0).astype(BF16)
             final = whole.at[i, here]
-            spread(i, lambda p: final, final, whole_ss, whole_rs.at[i])
+            spread(i, lambda p, g: final, final, whole_ss, whole_rs.at[i])
         for i in range(2):
             with jax.named_scope(f"whole_wait{i}"):
-                arrived(whole.at[i, pl.ds(0, side - 1)], whole_rs.at[i])
+                arrived(whole.at[i, pl.ds(0, spots - 1)], whole_rs.at[i])
             last(i).start()
         for i in range(2):
             lay_out(whole, out_weight_ref, i)
         take_back()
-        arrived(part_recv.at[:, pl.ds(0, side - 1)], part_ss)
+        arrived(part_recv.at[:, pl.ds(0, spots - 1)], part_ss)
         arrived(line_recv.at[:, pl.ds(0, side - 1)], line_ss)
-        arrived(cross_recv.at[:, pl.ds(0, n_group - 1)], cross_ss)
-        arrived(whole.at[:, pl.ds(0, side - 1)], whole_ss)
+        arrived(whole.at[:, pl.ds(0, spots - 1)], whole_ss)
         arrived(whole, pair_ss)
 
     @pl.when(core == 0)
@@ -415,14 +404,11 @@
         if WAIT[0]:
             pl.delay(WAIT[0])
         send_back(0, 0)
-        with jax.named_scope("tick_wait0"):
+        with jax.named_scope("tick_wait"):
             pl.semaphore_wait(tick, 1)
         if WAIT[1]:
             pl.delay(WAIT[1])
         send_back(0, 1)
-        with jax.named_scope("tick_wait1"):
-            pl.semaphore_wait(tick, 1)
-        send_back(0, 2)
         take_back()
         for i in range(2):
             with jax.named_scope(f"last_wait{i}"):
@@ -462,7 +448,7 @@
     dma = pltpu.SemaphoreType.DMA
     two = pltpu.SemaphoreType.DMA((2,))
     side = math.isqrt(chips)
-    part = (2, side, lines // (2 * side), LANES)
+    part = (2, side * n_group, lines // (2 * side * n_group), LANES)
     hbm = pl.BlockSpec(memory_space=pl.ANY)
     own_rows, terms, losses = pl.pallas_call(
         functools.partial(kernel, n, n_group),
@@ -497,15 +483,13 @@
             pltpu.VMEM(part, BF16),
             pltpu.VMEM(part, BF16),
             pltpu.VMEM((2, *part[2:]), BF16),
-            pltpu.VMEM(part, BF16),
-            pltpu.VMEM((2, *part[2:]), BF16),
-            pltpu.VMEM((2, n_group, *part[2:]), BF16),
+            pltpu.VMEM((2, side, *part[2:]), BF16),
             pltpu.VMEM(part, BF16),
             pltpu.SemaphoreType.DMA((4,)),
         ]
         + [dma, two] * 3
         + [dma, dma]
-        + [dma, two] * 5
+        + [dma, two] * 4
         + [pltpu.SemaphoreType.REGULAR],
         compiler_params=pltpu.CompilerParams(collective_id=0, has_side_effects=True),
         name="episodes",

time: 55.5 us -> 53.1 us (0.957)
  Pallas kernels: 54 us -> 51.7 us
    pallas_call x1, Pallas kernels: 52.4 us -> 50 us  [on_device(): pl.pallas_call(functools.partial(kernel, n, n_group), out_shape=(pltpu.VM...]
where the time goes in v5:
time: 53.1 us; the launch traced here: 53 us
  Pallas kernels  51.7 us (97%)
  between operations  1.29 us (2%)
    pallas_call x1, Pallas kernels, on_device(): pl.pallas_call(functools.partial(kernel, n, n_group), out_shape=(pltpu.VM...  50 us
    pallas_call x1, Pallas kernels, on_device(): pl.pallas_call(put_out, out_shape=(jax.ShapeDtypeStruct((rows, D), BF16),...  1.66 us

profile of v5, /device:TPU:1, one launch (start us, length us, event | category | flops | bytes accessed | tf_op | source)
XLA Modules:
  0.0 53.0 jit_solution(9980129409359113096)
XLA Ops:
  1.3 50.0 %episodes.1 = (bf16[128,512]{1,0:T(8,128)(2,1)S(1)}, f32[512,512]{1,0:T(8,128)S(1)}, f32[1,1]{1,0:T(1,128)}) custom-call(s32[1,128]{1,0:T(1,128)} %bitcast.6, s32[1,128]{1,0:T(1,128)} %bitcast.7, s32[1,128]{1,0:T(1,128)} %bitcast.8, s32[1,1]{1,0:T(1,128)} %bitcast.5.ways_hbm, bf16[128,512]{1,0:T(8,128)(2,1)} %features_hbm.1, bf16[512,512]{1,0:T(8,128)(2,1)} %weight_hbm.1), custom_call_target="tpu_custom_call" | custom-call | tf_op jit(solution)/shard_map/episodes/pallas_call | solution.py:453
  51.3 1.7 %results.1 = (bf16[128,512]{1,0:T(8,128)(2,1)}, f32[512,512]{1,0:T(8,128)}, f32[1,1]{1,0:T(1,128)}) custom-call(bf16[128,512]{1,0:T(8,128)(2,1)S(1)} %get-tuple-element.9.rows_ref, f32[512,512]{1,0:T(8,128)S(1)} %get-tuple-element.10.terms_ref, f32[1,1]{1,0:T(1,128)} %get-tuple-element.11.loss_ref), custom_call_target="tpu_custom_call" | custom-call | tf_op jit(solution)/shard_map/results/pallas_call | solution.py:504

commit v6 on v5

--- a/solution.py
+++ b/solution.py
@@ -340,16 +340,22 @@
         out_rows_ref[...] = dot(hot, returned, 0, 0).astype(BF16)
 
     def spread(axis, source, target, send_sem, recv_sem):
-        for place, peer in lines[axis][1] + [(lines[axis][0], me)]:
-            for other in groups + [group] * (peer is not me):
-                pltpu.make_async_remote_copy(
-                    src_ref=source(place, other),
-                    dst_ref=target,
-                    send_sem=send_sem,
-                    recv_sem=recv_sem,
-                    device_id=(peer, other),
-                    device_id_type=MESH,
-                ).start()
+        places = lines[axis][1] + [(lines[axis][0], me)]
+        shifts = [i for i in offsets if i] + [0]
+        pairs = [(p, g) for p in range(side) for g in range(n_group) if shifts[p] or g]
+        hops = lambda i, count: min(i, count - i)
+        pairs.sort(key=lambda pair: -hops(shifts[pair[0]], side) - hops(pair[1], n_group))
+        for p, g in pairs:
+            place, peer = places[p]
+            other = ([group] + groups)[g]
+            pltpu.make_async_remote_copy(
+                src_ref=source(place, other),
+                dst_ref=target,
+                send_sem=send_sem,
+                recv_sem=recv_sem,
+                device_id=(peer, other),
+                device_id_type=MESH,
+            ).start()
 
     def tell():
         pl.semaphore_signal(tick, inc=1, device_id=(twin, group), device_id_type=MESH)

time: 53.1 us -> 52.9 us (level)
  no operation moved by 1% of the time
where the time goes in v6:
time: 52.9 us; the launch traced here: 52.8 us
  Pallas kernels  51.5 us (97%)
  between operations  1.29 us (2%)
    pallas_call x1, Pallas kernels, on_device(): pl.pallas_call(functools.partial(kernel, n, n_group), out_shape=(pltpu.VM...  49.8 us
    pallas_call x1, Pallas kernels, on_device(): pl.pallas_call(put_out, out_shape=(jax.ShapeDtypeStruct((rows, D), BF16),...  1.66 us

profile of v6, /device:TPU:1, one launch (start us, length us, event | category | flops | bytes accessed | tf_op | source)
XLA Modules:
  0.0 52.8 jit_solution(4392251142042851157)
XLA Ops:
  1.3 49.8 %episodes.1 = (bf16[128,512]{1,0:T(8,128)(2,1)S(1)}, f32[512,512]{1,0:T(8,128)S(1)}, f32[1,1]{1,0:T(1,128)}) custom-call(s32[1,128]{1,0:T(1,128)} %bitcast.6, s32[1,128]{1,0:T(1,128)} %bitcast.7, s32[1,128]{1,0:T(1,128)} %bitcast.8, s32[1,1]{1,0:T(1,128)} %bitcast.5.ways_hbm, bf16[128,512]{1,0:T(8,128)(2,1)} %features_hbm.1, bf16[512,512]{1,0:T(8,128)(2,1)} %weight_hbm.1), custom_call_target="tpu_custom_call" | custom-call | tf_op jit(solution)/shard_map/episodes/pallas_call | solution.py:459
  51.1 1.7 %results.1 = (bf16[128,512]{1,0:T(8,128)(2,1)}, f32[512,512]{1,0:T(8,128)}, f32[1,1]{1,0:T(1,128)}) custom-call(bf16[128,512]{1,0:T(8,128)(2,1)S(1)} %get-tuple-element.9.rows_ref, f32[512,512]{1,0:T(8,128)S(1)} %get-tuple-element.10.terms_ref, f32[1,1]{1,0:T(1,128)} %get-tuple-element.11.loss_ref), custom_call_target="tpu_custom_call" | custom-call | tf_op jit(solution)/shard_map/results/pallas_call | solution.py:510
